TPU v7x, 8 devices: a whole 2x2x1 slice. The times are simulated.
8 devices in a mesh: dp: 1 (over z), tp: 8 (over y, x, core).
Axes of the slice: x: 2, y: 2, z: 1, core: 2. Of those that a mesh axis runs over, the one named last changes fastest.
Arguments:
- hidden: bfloat16 [512, 2048], P('dp')
- w_query: bfloat16 [2048, 2048], P(None, 'tp')
- w_key: bfloat16 [2048, 256], replicated
- w_value: bfloat16 [2048, 256], replicated
- w_out: bfloat16 [2048, 2048], P('tp')
- k_cache: bfloat16 [512, 512, 256], P(('dp', 'tp'))
- v_cache: bfloat16 [512, 512, 256], P(('dp', 'tp'))
- lengths: int32 [512], P('dp')
Outputs:
- output 1: bfloat16 [512, 2048], P('dp', 'tp')
- output 2: bfloat16 [512, 512, 256], P(('dp', 'tp'))
- output 3: bfloat16 [512, 512, 256], P(('dp', 'tp'))
All inputs are finite; a program needn't handle non-finite values.
Results may differ from a plain program's by a relative error of at most 0.0162064.
Values are sent between devices in bfloat16 or wider.
A program may use at most 1 GiB of HBM per device.

v0:
```python
import jax
import jax.numpy as jnp
from jax import lax
from jax.sharding import PartitionSpec as P


def rope_angles(positions, head_dim):
    half_dim = head_dim // 2
    inv_freq = 10000.0 ** (-(jnp.arange(half_dim, dtype=jnp.float32) * 2.0) / head_dim)
    return positions.astype(jnp.float32)[:, None] * inv_freq[None, :]


def apply_rope(values_in, angles):
    half_dim = values_in.shape[-1] // 2
    first_half = values_in[..., :half_dim]
    second_half = values_in[..., half_dim:]
    cosines = jnp.cos(angles)
    sines = jnp.sin(angles)
    return jnp.concatenate([first_half * cosines - second_half * sines, second_half * cosines + first_half * sines], axis=-1)


def attend(q_rot, k_all, v_all, lengths):
    head_dim = q_rot.shape[-1]
    seq_len = k_all.shape[1]
    scores = jnp.einsum('bhd,bsd->bhs', q_rot, k_all, preferred_element_type=jnp.float32) * (head_dim ** -0.5)
    valid_mask = lax.broadcasted_iota(jnp.int32, (1, 1, seq_len), 2) <= lengths[:, None, None]
    scores = jnp.where(valid_mask, scores, -1e30)
    row_max = jnp.max(scores, axis=-1, keepdims=True)
    weights = jnp.exp(scores - row_max)
    denominator = jnp.sum(weights, axis=-1, keepdims=True)
    summed = jnp.einsum('bhs,bsd->bhd', weights.astype(jnp.bfloat16), v_all, preferred_element_type=jnp.float32)
    return (summed / denominator).astype(jnp.bfloat16)


def solution(mesh):
    group_size = mesh.shape['tp']
    cache_spec = P(('dp', 'tp'), None, None)

    def local_step(hidden, w_query, w_key, w_value, w_out, k_cache, v_cache, lengths):
        rows_dev, seq_len, head_dim = k_cache.shape
        cols_dev = w_query.shape[1]
        num_heads = cols_dev * group_size // head_dim
        row_start = lax.axis_index('tp') * rows_dev
        q_cols = jnp.dot(hidden, w_query, preferred_element_type=jnp.float32).astype(jnp.bfloat16)
        q_rows = lax.all_to_all(q_cols, 'tp', 0, 1, tiled=True)
        own_hidden = lax.dynamic_slice_in_dim(hidden, row_start, rows_dev, axis=0)
        own_lengths = lax.dynamic_slice_in_dim(lengths, row_start, rows_dev, axis=0)
        k_new = jnp.dot(own_hidden, w_key, preferred_element_type=jnp.float32).astype(jnp.bfloat16)
        v_new = jnp.dot(own_hidden, w_value, preferred_element_type=jnp.float32).astype(jnp.bfloat16)
        angles = rope_angles(own_lengths, head_dim)
        q_heads = q_rows.reshape(rows_dev, num_heads, head_dim).astype(jnp.float32)
        q_rot = apply_rope(q_heads, angles[:, None, :]).astype(jnp.bfloat16)
        k_rot = apply_rope(k_new.astype(jnp.float32), angles).astype(jnp.bfloat16)
        new_slot = (lax.broadcasted_iota(jnp.int32, (1, seq_len), 1) == own_lengths[:, None])[:, :, None]
        k_out = jnp.where(new_slot, k_rot[:, None, :], k_cache)
        v_out = jnp.where(new_slot, v_new[:, None, :], v_cache)
        attn_out = attend(q_rot, k_out, v_out, own_lengths)
        o_cols = lax.all_to_all(attn_out.reshape(rows_dev, num_heads * head_dim), 'tp', 1, 0, tiled=True)
        y_part = jnp.dot(o_cols, w_out, preferred_element_type=jnp.float32).astype(jnp.bfloat16)
        y_local = lax.psum_scatter(y_part, 'tp', scatter_dimension=1, tiled=True)
        return y_local, k_out, v_out

    return jax.shard_map(
        local_step,
        mesh=mesh,
        in_specs=(P('dp', None), P(None, 'tp'), P(), P(), P('tp', None), cache_spec, cache_spec, P('dp')),
        out_specs=(P('dp', 'tp'), cache_spec, cache_spec),
        check_vma=False,
    )
```

profile of v0, /device:TPU:0, one launch (start us, length us, event | category | flops | bytes accessed | tf_op | source)
XLA Modules:
  0.0 112.6 jit_solution(9858954959199783894)
XLA Ops:
  7.2 0.0 copy-start
  7.2 1.6 %copy-done = bf16[512,2048]{1,0:T(8,128)(2,1)S(1)} copy-done((bf16[512,2048]{1,0:T(8,128)(2,1)S(1)}, bf16[512,2048]{1,0:T(8,128)(2,1)}, u32[]{:S(2)}) %copy-start) | copy-done | bytes 2097176
  8.8 2.6 %convolution_convert_fusion.1 = bf16[512,256]{1,0:T(8,128)(2,1)} fusion(bf16[512,2048]{1,0:T(8,128)(2,1)S(1)} %copy-done, bf16[2048,256]{1,0:T(8,128)(2,1)} %param.9), kind=kOutput, calls=%fused_computation.7 | convolution fusion | flops 537001984 | bytes 3407872 | tf_op jit(solution)/shard_map/dot_general | solution.py:44
  11.4 4.3 %all-to-all-start = ((bf16[8,64,256]{2,1,0:T(8,128)(2,1)}), bf16[8,64,256]{2,1,0:T(8,128)(2,1)S(1)}, u32[]{:S(2)}, u32[]{:S(2)}) async-start(bf16[8,64,256]{2,1,0:T(8,128)(2,1)} %bitcast), calls=%async_computation | async-start | bytes 524288 | tf_op jit(solution)/shard_map/all_to_all | solution.py:45
  15.7 0.0 reduce-scatter.2.cloned.1.call-start
  15.8 0.8 fusion.15
  16.5 1.5 %convolution_convert_fusion.2 = bf16[64,256]{1,0:T(8,128)(2,1)S(1)} fusion(bf16[2048,256]{1,0:T(8,128)(2,1)} %param.11, bf16[512,2048]{1,0:T(8,128)(2,1)S(1)} %copy-done, s32[]{:T(128)S(6)} %select_n.15), kind=kOutput, calls=%fused_computation.8 | convolution fusion | flops 67125248 | bytes 1343492 | tf_op jit(solution)/shard_map/dot_general | solution.py:49
  18.1 1.5 %fusion.2 = f32[64,256]{1,0:T(8,128)S(1)} fusion(bf16[2048,256]{1,0:T(8,128)(2,1)} %param.10, bf16[512,2048]{1,0:T(8,128)(2,1)S(1)} %copy-done, s32[]{:T(128)S(6)} %select_n.15), kind=kOutput, calls=%fused_computation.10 | convolution fusion | flops 67141632 | bytes 1376260 | tf_op jit(solution)/shard_map/dot_general | solution.py:48
  19.6 0.1 iota_compare_fusion.1
  19.7 0.2 multiply_cosine_fusion
  19.9 23.1 %broadcast_select_fusion.1 = (bf16[64,512,256]{2,1,0:T(8,128)(2,1)}, bf16[64,512,256]{2,1,0:T(8,128)(2,1)}) fusion(bf16[64,512,256]{2,1,0:T(8,128)(2,1)} %param.13, pred[64,512]{1,0:T(8,128)(4,1)S(1)} %get-tuple-element.16, bf16[64,256]{1,0:T(8,128)(2,1)S(1)} %pad_maximum_fusion, bf16[64,512,256]{2,1,0:T(8,128)(2,1)} %param.14, ...), kind=kLoop, calls=%fused_computation.1 | loop fusion | flops 16777216 | bytes 67207168 | tf_op jit(solution)/shard_map/jit(_where)/select_n | solution.py:55
  43.0 0.0 all-to-all-done
  43.0 0.2 convert_bitcast_fusion
  43.2 0.1 subtract_convert_fusion
  43.3 10.3 %fusion.16 = (f32[64,8]{1,0:T(8,128)S(1)}, f32[64,8,512]{2,1,0:T(8,128)S(1)}) fusion(bf16[64,512,256]{2,1,0:T(8,128)(2,1)} %get-tuple-element.9, bf16[64,8,128]{2,1,0:T(8,128)(2,1)S(1)} %get-tuple-element.6, bf16[64,8,128]{2,1,0:T(8,128)(2,1)S(1)} %get-tuple-element.5, pred[64,512]{1,0:T(8,128)(4,1)S(1)} %get-tuple-element.15), kind=kOutput, calls=%fused_computation.35 | convolution fusion | flops 135527936 | bytes 18122752 | tf_op jit(solution)/shard_map/bhd,bsd->bhs/dot_general | solution.py:25
  53.5 0.0 copy-start.2
  53.5 0.3 fusion.3
  53.9 0.0 copy-start.1
  53.9 8.3 %fusion.1 = bf16[64,8,256]{2,1,0:T(8,128)(2,1)S(1)} fusion(bf16[64,512,256]{2,1,0:T(8,128)(2,1)} %get-tuple-element.10, f32[64,8,512]{2,1,0:T(8,128)S(1)} %get-tuple-element.18, f32[64,8]{1,0:T(8,128)S(1)} %get-tuple-element.17, f32[64,8]{1,0:T(8,128)S(1)} %fusion.3), kind=kOutput, calls=%fused_computation.6 | convolution fusion | flops 135004160 | bytes 18092032 | tf_op jit(solution)/shard_map/bhs,bsd->bhd/dot_general | solution.py:31
  62.1 0.1 copy.15
  62.2 9.6 %all_to_all.29 = bf16[64,8,256]{2,0,1:T(8,128)(2,1)S(1)} all-to-all(bf16[64,8,256]{2,0,1:T(8,128)(2,1)S(1)} %copy.15), channel_id=1, replica_groups=mesh['dp'=1,'tp'=8] {'tp'}, dimensions={1} | all-to-all | bytes 524288 | tf_op jit(solution)/shard_map/all_to_all | solution.py:58
  71.8 0.0 copy-done.2
  71.8 2.1 %convolution_convert_fusion = bf16[512,2048]{1,0:T(8,128)(2,1)} fusion(bf16[512,256]{1,0:T(8,128)(2,1)S(1)} %bitcast.14, bf16[256,2048]{1,0:T(8,128)(2,1)S(1)} %copy-done.2), kind=kOutput, calls=%fused_computation.2 | convolution fusion | flops 537919488 | bytes 3407872 | tf_op jit(solution)/shard_map/dot_general | solution.py:59
  73.9 0.0 reduce-scatter.2.cloned.1.call-update
  73.9 31.8 %reduce-scatter.2.cloned.1.call-done = bf16[512,256]{1,0:T(8,128)(2,1)} async-done(((bf16[512,2048]{1,0:T(8,128)(2,1)}), bf16[512,256]{1,0:T(8,128)(2,1)}) %reduce-scatter.2.cloned.1.call-update) | async-done | bytes 262160 | tf_op jit(solution)/shard_map/reduce_scatter | solution.py:60
  105.7 0.0 copy-done.1
  (2 shorter events, 0.0 us)
Async XLA Ops:
  7.2 1.6 %copy-start = (bf16[512,2048]{1,0:T(8,128)(2,1)S(1)}, bf16[512,2048]{1,0:T(8,128)(2,1)}, u32[]{:S(2)}) copy-start(bf16[512,2048]{1,0:T(8,128)(2,1)} %param.8) | copy-start | bytes 6291460
  11.4 31.6 %all-to-all-start = ((bf16[8,64,256]{2,1,0:T(8,128)(2,1)}), bf16[8,64,256]{2,1,0:T(8,128)(2,1)S(1)}, u32[]{:S(2)}, u32[]{:S(2)}) async-start(bf16[8,64,256]{2,1,0:T(8,128)(2,1)} %bitcast), calls=%async_computation | async-start | bytes 524288 | tf_op jit(solution)/shard_map/all_to_all | solution.py:45
  15.7 90.0 %reduce-scatter.2.cloned.1.call-start = ((), (), s32[]{:S(2)}) async-start(), calls=%async_computation.3 | async-start | bytes 2359296 | tf_op jit(solution)/shard_map/reduce_scatter | solution.py:60
  53.5 18.3 %copy-start.2 = (bf16[256,2048]{1,0:T(8,128)(2,1)S(1)}, bf16[256,2048]{1,0:T(8,128)(2,1)}, u32[]{:S(2)}) copy-start(bf16[256,2048]{1,0:T(8,128)(2,1)} %param.12) | copy-start | bytes 3145732
  53.9 51.9 %copy-start.1 = (bf16[512,2048]{1,0:T(8,128)(2,1)S(1)}, bf16[512,2048]{1,0:T(8,128)(2,1)}, u32[]{:S(2)}) copy-start(bf16[512,2048]{1,0:T(8,128)(2,1)} %param.8) | copy-start | bytes 6291460
Sparse Core Ops, SparseCore 0:
  74.0 31.6 reduce-scatter.1
where the time goes:
time: 113 us
  waiting for transfers between devices  31.8 us (28%)
  matrix products  26.3 us (23%)
  other arithmetic  24.7 us (22%)
  between operations  14.1 us (12%)
  blocking collectives  9.58 us (8%)
  starting transfers between devices  4.34 us (4%)
  local copies, waits for them, and re-layouts  1.66 us (1%)
    reduce_scatter x1, waiting for transfers between devices, local_step(): y_local = lax.psum_scatter(y_part, 'tp', scatter_dimension=1, tiled=True)  31.8 us
    select_n x1, other arithmetic, local_step(): k_out = jnp.where(new_slot, k_rot[:, None, :], k_cache)  23.1 us
    dot_general x1, matrix products, attend(): jnp.einsum('bhd,bsd->bhs', q_rot, k_all, preferred_element_type=jnp.float32)  10.3 us
    all_to_all x1, blocking collectives, local_step(): lax.all_to_all(attn_out.reshape(rows_dev, num_heads * head_dim), 'tp', 1,...  9.58 us
    dot_general x1, matrix products, attend(): jnp.einsum('bhs,bsd->bhd', weights.astype(jnp.bfloat16), v_all, preferred...  8.27 us
    all_to_all x1, starting transfers between devices, local_step(): q_rows = lax.all_to_all(q_cols, 'tp', 0, 1, tiled=True)  4.31 us
    dot_general x1, matrix products, local_step(): jnp.dot(hidden, w_query, preferred_element_type=jnp.float32)  2.64 us
  transfers between devices with their start and end apart: 2, of which 1 were waited for; matrix products, arithmetic and copies ran while one was open for 24% of the time, Pallas kernels for 0%

commit v1 on v0

--- a/solution.py
+++ b/solution.py
@@ -40,7 +40,18 @@
         rows_dev, seq_len, head_dim = k_cache.shape
         cols_dev = w_query.shape[1]
         num_heads = cols_dev * group_size // head_dim
-        row_start = lax.axis_index('tp') * rows_dev
+        me = lax.axis_index('tp')
+        row_start = me * rows_dev
+
+        def swap(value, mask):
+            return lax.ppermute(value, 'tp', [(i, i ^ mask) for i in range(group_size)])
+
+        blocks = w_out.reshape(cols_dev, group_size, cols_dev).transpose(1, 0, 2)
+        w_cols = jnp.zeros((group_size, cols_dev, cols_dev), w_out.dtype)
+        for mask in range(group_size):
+            block = lax.dynamic_index_in_dim(blocks, me ^ mask, 0, keepdims=True)
+            w_cols = lax.dynamic_update_slice(w_cols, swap(block, mask) if mask else block, (me ^ mask, 0, 0))
+        w_cols = w_cols.reshape(group_size * cols_dev, cols_dev)
         q_cols = jnp.dot(hidden, w_query, preferred_element_type=jnp.float32).astype(jnp.bfloat16)
         q_rows = lax.all_to_all(q_cols, 'tp', 0, 1, tiled=True)
         own_hidden = lax.dynamic_slice_in_dim(hidden, row_start, rows_dev, axis=0)
@@ -55,9 +66,15 @@
         k_out = jnp.where(new_slot, k_rot[:, None, :], k_cache)
         v_out = jnp.where(new_slot, v_new[:, None, :], v_cache)
         attn_out = attend(q_rot, k_out, v_out, own_lengths)
-        o_cols = lax.all_to_all(attn_out.reshape(rows_dev, num_heads * head_dim), 'tp', 1, 0, tiled=True)
-        y_part = jnp.dot(o_cols, w_out, preferred_element_type=jnp.float32).astype(jnp.bfloat16)
-        y_local = lax.psum_scatter(y_part, 'tp', scatter_dimension=1, tiled=True)
+        o_own = attn_out.reshape(rows_dev, num_heads * head_dim)
+        chips = [o_own] + [swap(o_own, mask) for mask in (2, 4, 6)]
+        half = jnp.stack(chips)
+        sibling = swap(half, 1)
+        o_all = jnp.concatenate([half, sibling]).reshape(group_size * rows_dev, num_heads * head_dim)
+        y_mask = jnp.dot(o_all, w_cols, preferred_element_type=jnp.float32).astype(jnp.bfloat16)
+        y_local = jnp.zeros((group_size * rows_dev, cols_dev), jnp.bfloat16)
+        for slot, mask in enumerate((0, 2, 4, 6, 1, 3, 5, 7)):
+            y_local = lax.dynamic_update_slice(y_local, y_mask[slot * rows_dev:(slot + 1) * rows_dev], ((me ^ mask) * rows_dev, 0))
         return y_local, k_out, v_out
 
     return jax.shard_map(

time: 113 us -> 102 us (0.903)
  local copies, waits for them, and re-layouts: 1.66 us -> 22.1 us
  waiting for transfers between devices: 31.8 us -> 12.7 us
  between operations: 14.1 us -> 1.13 us
  starting transfers between devices: 4.34 us -> 14.4 us
  blocking collectives: 9.58 us -> 0 us
  other arithmetic: 24.7 us -> 26.4 us
  matrix products: 26.3 us -> 24.8 us
    reduce_scatter x1 -> x0, waiting for transfers between devices: 31.8 us -> none  [local_step(): y_local = lax.psum_scatter(y_part, 'tp', scatter_dimension=1, tiled=True)]
    ppermute x0 -> x11, waiting for transfers between devices: none -> 12.7 us  [swap(): return lax.ppermute(value, 'tp', [(i, i ^ mask) for i in range(group_size)])]
    another operation x0 -> x10, local copies, waits for them, and re-layouts: none -> 10.7 us
    ppermute x0 -> x11, starting transfers between devices: none -> 10.1 us  [swap(): return lax.ppermute(value, 'tp', [(i, i ^ mask) for i in range(group_size)])]
    all_to_all x1 -> x0, blocking collectives: 9.58 us -> none  [local_step(): lax.all_to_all(attn_out.reshape(rows_dev, num_heads * head_dim), 'tp', 1,...]
    unnamed x6 -> x22, local copies, waits for them, and re-layouts: 1.6 us -> 6.6 us
    dynamic_update_slice x0 -> x16, local copies, waits for them, and re-layouts: none -> 4.71 us  [the longest x8 4.63 us: local_step(): lax.dynamic_update_slice(w_cols, swap(block, mask) if mask else block, (m...]
    dot_general x1, matrix products: 2.06 us -> 0.71 us  [local_step(): jnp.dot(o_all, w_cols, preferred_element_type=jnp.float32)]
  transfers between devices with their start and end apart: 2 -> 12, of which waited for: 1 -> 3; matrix products, arithmetic and copies ran while one was open for 24% -> 66% of each run, Pallas kernels for 0% -> 0%
where the time goes in v1:
time: 102 us
  other arithmetic  26.4 us (26%)
  matrix products  24.8 us (24%)
  local copies, waits for them, and re-layouts  22.1 us (22%)
  starting transfers between devices  14.4 us (14%)
  waiting for transfers between devices  12.7 us (12%)
  between operations  1.13 us (1%)
    select_n x1, other arithmetic, local_step(): k_out = jnp.where(new_slot, k_rot[:, None, :], k_cache)  23.3 us
    ppermute x11, waiting for transfers between devices, swap(): return lax.ppermute(value, 'tp', [(i, i ^ mask) for i in range(group_size)])  12.7 us
    another operation x9, local copies, waits for them, and re-layouts  10.5 us
    dot_general x1, matrix products, attend(): jnp.einsum('bhd,bsd->bhs', q_rot, k_all, preferred_element_type=jnp.float32)  10.3 us
    ppermute x11, starting transfers between devices, swap(): return lax.ppermute(value, 'tp', [(i, i ^ mask) for i in range(group_size)])  10.1 us
    dot_general x1, matrix products, attend(): jnp.einsum('bhs,bsd->bhd', weights.astype(jnp.bfloat16), v_all, preferred...  8.12 us
    unnamed x22, local copies, waits for them, and re-layouts  6.6 us
    dynamic_update_slice x8, local copies, waits for them, and re-layouts, local_step(): lax.dynamic_update_slice(w_cols, swap(block, mask) if mask else block, (m...  4.63 us
  transfers between devices with their start and end apart: 12, of which 3 were waited for; matrix products, arithmetic and copies ran while one was open for 66% of the time, Pallas kernels for 0%

profile of v1, /device:TPU:0, one launch (start us, length us, event | category | flops | bytes accessed | tf_op | source)
XLA Modules:
  0.0 101.7 jit_solution(10274355112384847839)
XLA Ops:
  0.6 1.6 %copy-done = bf16[512,2048]{1,0:T(8,128)(2,1)S(1)} copy-done((bf16[512,2048]{1,0:T(8,128)(2,1)S(1)}, bf16[512,2048]{1,0:T(8,128)(2,1)}, u32[]{:S(2)}) %copy-start) | copy-done | bytes 2097176
  2.2 2.6 %convolution_convert_fusion.1 = bf16[512,256]{1,0:T(8,128)(2,1)} fusion(bf16[512,2048]{1,0:T(8,128)(2,1)S(1)} %copy-done, bf16[2048,256]{1,0:T(8,128)(2,1)} %param.9), kind=kOutput, calls=%fused_computation.7 | convolution fusion | flops 537001984 | bytes 3407872 | tf_op jit(solution)/shard_map/dot_general | solution.py:55
  4.9 4.3 %all-to-all-start = ((bf16[8,64,256]{2,1,0:T(8,128)(2,1)}), bf16[8,64,256]{2,1,0:T(8,128)(2,1)S(1)}, u32[]{:S(2)}, u32[]{:S(2)}) async-start(bf16[8,64,256]{2,1,0:T(8,128)(2,1)} %bitcast), calls=%async_computation | async-start | bytes 524288 | tf_op jit(solution)/shard_map/all_to_all | solution.py:56
  9.2 1.5 %copy.24 = bf16[256,2048]{0,1:T(8,128)(2,1)S(1)} copy(bf16[256,2048]{1,0:T(8,128)(2,1)} %param.12) | data formatting | bytes 2097152 | tf_op args[4]
  10.7 0.9 constant_dynamic-slice_fusion
  11.6 1.7 %copy.26 = bf16[256,1,256]{2,0,1:T(8,128)(2,1)} copy(bf16[256,1,256]{0,2,1:T(8,128)(2,1)} %get-tuple-element.11) | data formatting | bytes 262144 | tf_op jit(solution)/shard_map/dynamic-slice.1
  13.9 1.7 %copy.27 = bf16[256,1,256]{2,0,1:T(8,128)(2,1)} copy(bf16[256,1,256]{0,2,1:T(8,128)(2,1)} %get-tuple-element.10) | data formatting | bytes 262144 | tf_op jit(solution)/shard_map/dynamic-slice.2
  15.5 1.6 %collective-permute-start.5 = (bf16[1,256,256]{2,1,0:T(8,128)(2,1)}, bf16[1,256,256]{2,1,0:T(8,128)(2,1)}, u32[]{:S(2)}, u32[]{:S(2)}) collective-permute-start(bf16[1,256,256]{2,1,0:T(8,128)(2,1)} %bitcast.43), channel_id=1, source_target_pairs={{0,2},{1,3},{2,0},{3,1},{4,6},{5,7},{6,4},{7,5}} | collective-permute-start | bytes 393224 | tf_op jit(solution)/shard_map/ppermute | solution.py:47
  17.2 1.7 %copy.28 = bf16[256,1,256]{2,0,1:T(8,128)(2,1)} copy(bf16[256,1,256]{0,2,1:T(8,128)(2,1)} %get-tuple-element.9) | data formatting | bytes 262144 | tf_op jit(solution)/shard_map/dynamic-slice.3
  18.8 1.7 %copy.29 = bf16[256,1,256]{2,0,1:T(8,128)(2,1)} copy(bf16[256,1,256]{0,2,1:T(8,128)(2,1)} %get-tuple-element.8) | data formatting | bytes 262144 | tf_op jit(solution)/shard_map/dynamic-slice.4
  20.5 1.7 %collective-permute-start.7 = (bf16[1,256,256]{2,1,0:T(8,128)(2,1)}, bf16[1,256,256]{2,1,0:T(8,128)(2,1)}, u32[]{:S(2)}, u32[]{:S(2)}) collective-permute-start(bf16[1,256,256]{2,1,0:T(8,128)(2,1)} %bitcast.41), channel_id=1, source_target_pairs={{0,4},{1,5},{2,6},{3,7},{4,0},{5,1},{6,2},{7,3}} | collective-permute-start | bytes 393224 | tf_op jit(solution)/shard_map/ppermute | solution.py:47
  22.3 1.7 %copy.30 = bf16[256,1,256]{2,0,1:T(8,128)(2,1)} copy(bf16[256,1,256]{0,2,1:T(8,128)(2,1)} %get-tuple-element.7) | data formatting | bytes 262144 | tf_op jit(solution)/shard_map/dynamic-slice.5
  24.0 0.8 fusion.15
  25.5 2.1 %fusion.2 = f32[64,256]{1,0:T(8,128)} fusion(bf16[2048,256]{1,0:T(8,128)(2,1)} %param.10, bf16[512,2048]{1,0:T(8,128)(2,1)S(1)} %copy-done, s32[]{:T(128)S(6)} %select_n.70), kind=kOutput, calls=%fused_computation.10 | convolution fusion | flops 67141632 | bytes 1376260 | tf_op jit(solution)/shard_map/dot_general | solution.py:59
  27.7 0.9 convolution_convert_fusion.2
  28.6 1.0 copy.25
  29.6 1.0 multiply_cosine_fusion
  30.6 23.3 %broadcast_select_fusion.1 = (bf16[64,512,256]{2,1,0:T(8,128)(2,1)}, bf16[64,512,256]{2,1,0:T(8,128)(2,1)}) fusion(bf16[64,512,256]{2,1,0:T(8,128)(2,1)} %param.13, pred[64,512]{1,0:T(8,128)(4,1)} %get-tuple-element.24, bf16[64,256]{1,0:T(8,128)(2,1)S(1)} %pad_maximum_fusion.1, bf16[64,512,256]{2,1,0:T(8,128)(2,1)} %param.14, ...), kind=kLoop, calls=%fused_computation.1 | loop fusion | flops 16777216 | bytes 67207168 | tf_op jit(solution)/shard_map/jit(_where)/select_n | solution.py:66
  54.3 2.6 %collective-permute-start.9 = (bf16[1,256,256]{2,1,0:T(8,128)(2,1)S(1)}, bf16[1,256,256]{2,1,0:T(8,128)(2,1)S(1)}, u32[]{:S(2)}, u32[]{:S(2)}) collective-permute-start(bf16[1,256,256]{2,1,0:T(8,128)(2,1)S(1)} %bitcast.46), channel_id=1, source_target_pairs={{0,6},{1,7},{2,4},{3,5},{4,2},{5,3},{6,0},{7,1}} | collective-permute-start | bytes 393224 | tf_op jit(solution)/shard_map/ppermute | solution.py:47
  56.9 0.9 constant_dynamic-update-slice_fusion.11
  57.9 0.9 constant_dynamic-update-slice_fusion.10
  58.8 0.9 constant_dynamic-update-slice_fusion.9
  59.7 0.9 constant_dynamic-update-slice_fusion.8
  60.7 0.9 constant_dynamic-update-slice_fusion.7
  61.9 10.3 %fusion.16 = (f32[64,8]{1,0:T(8,128)S(1)}, f32[64,8,512]{2,1,0:T(8,128)S(1)}) fusion(bf16[64,512,256]{2,1,0:T(8,128)(2,1)} %get-tuple-element.17, bf16[64,8,128]{2,1,0:T(8,128)(2,1)S(1)} %get-tuple-element.14, bf16[64,8,128]{2,1,0:T(8,128)(2,1)S(1)} %get-tuple-element.13, pred[64,512]{1,0:T(8,128)(4,1)S(1)} %copy-done.7), kind=kOutput, calls=%fused_computation.65 | convolution fusion | flops 135527936 | bytes 18122752 | tf_op jit(solution)/shard_map/bhd,bsd->bhs/dot_general | solution.py:25
  72.5 8.1 %fusion.1 = bf16[64,8,256]{2,1,0:T(8,128)(2,1)S(1)} fusion(bf16[64,512,256]{2,1,0:T(8,128)(2,1)} %get-tuple-element.18, f32[64,8,512]{2,1,0:T(8,128)S(1)} %get-tuple-element.26, f32[64,8]{1,0:T(8,128)S(1)} %get-tuple-element.25, f32[64,8]{1,0:T(8,128)S(1)} %fusion.3), kind=kOutput, calls=%fused_computation.5 | convolution fusion | flops 135004160 | bytes 18092032 | tf_op jit(solution)/shard_map/bhs,bsd->bhd/dot_general | solution.py:31
  80.7 1.8 %collective-permute-start = (bf16[64,2048]{1,0:T(8,128)(2,1)S(1)}, bf16[64,2048]{1,0:T(8,128)(2,1)S(1)}, u32[]{:S(2)}, u32[]{:S(2)}) collective-permute-start(bf16[64,2048]{1,0:T(8,128)(2,1)S(1)} %bitcast.37), channel_id=1, source_target_pairs={{0,2},{1,3},{2,0},{3,1},{4,6},{5,7},{6,4},{7,5}} | collective-permute-start | bytes 786440 | tf_op jit(solution)/shard_map/ppermute | solution.py:47
  82.5 1.4 %collective-permute-start.1 = (bf16[64,2048]{1,0:T(8,128)(2,1)S(1)}, bf16[64,2048]{1,0:T(8,128)(2,1)S(1)}, u32[]{:S(2)}, u32[]{:S(2)}) collective-permute-start(bf16[64,2048]{1,0:T(8,128)(2,1)S(1)} %bitcast.38), channel_id=1, source_target_pairs={{0,4},{1,5},{2,6},{3,7},{4,0},{5,1},{6,2},{7,3}} | collective-permute-start | bytes 786440 | tf_op jit(solution)/shard_map/ppermute | solution.py:47
  84.4 5.5 %collective-permute-done = bf16[64,2048]{1,0:T(8,128)(2,1)S(1)} collective-permute-done((bf16[64,2048]{1,0:T(8,128)(2,1)S(1)}, bf16[64,2048]{1,0:T(8,128)(2,1)S(1)}, u32[]{:S(2)}, u32[]{:S(2)}) %collective-permute-start) | collective-permute-done | bytes 262176 | tf_op jit(solution)/shard_map/ppermute | solution.py:47
  89.9 6.5 %collective-permute-done.1 = bf16[64,2048]{1,0:T(8,128)(2,1)S(1)} collective-permute-done((bf16[64,2048]{1,0:T(8,128)(2,1)S(1)}, bf16[64,2048]{1,0:T(8,128)(2,1)S(1)}, u32[]{:S(2)}, u32[]{:S(2)}) %collective-permute-start.1) | collective-permute-done | bytes 262176 | tf_op jit(solution)/shard_map/ppermute | solution.py:47
  97.4 1.0 constant_dynamic-update-slice_fusion.2
  98.3 1.0 constant_dynamic-update-slice_fusion.1
  (59 shorter events, 6.0 us)
Async XLA Ops:
  0.6 1.6 %copy-start = (bf16[512,2048]{1,0:T(8,128)(2,1)S(1)}, bf16[512,2048]{1,0:T(8,128)(2,1)}, u32[]{:S(2)}) copy-start(bf16[512,2048]{1,0:T(8,128)(2,1)} %param.8) | copy-start | bytes 6291460
  4.9 56.8 %all-to-all-start = ((bf16[8,64,256]{2,1,0:T(8,128)(2,1)}), bf16[8,64,256]{2,1,0:T(8,128)(2,1)S(1)}, u32[]{:S(2)}, u32[]{:S(2)}) async-start(bf16[8,64,256]{2,1,0:T(8,128)(2,1)} %bitcast), calls=%async_computation | async-start | bytes 524288 | tf_op jit(solution)/shard_map/all_to_all | solution.py:56
  11.6 16.1 %copy-start.2 = (bf16[2048,256]{1,0:T(8,128)(2,1)S(1)}, bf16[2048,256]{1,0:T(8,128)(2,1)}, u32[]{:S(2)}) copy-start(bf16[2048,256]{1,0:T(8,128)(2,1)} %param.11) | copy-start | bytes 3145732
  13.4 40.9 %collective-permute-start.4 = (bf16[1,256,256]{2,1,0:T(8,128)(2,1)}, bf16[1,256,256]{2,1,0:T(8,128)(2,1)}, u32[]{:S(2)}, u32[]{:S(2)}) collective-permute-start(bf16[1,256,256]{2,1,0:T(8,128)(2,1)} %bitcast.44), channel_id=1, source_target_pairs={{0,1},{1,0},{2,3},{3,2},{4,5},{5,4},{6,7},{7,6}} | collective-permute-start | bytes 393224 | tf_op jit(solution)/shard_map/ppermute | solution.py:47
  15.5 42.3 %collective-permute-start.5 = (bf16[1,256,256]{2,1,0:T(8,128)(2,1)}, bf16[1,256,256]{2,1,0:T(8,128)(2,1)}, u32[]{:S(2)}, u32[]{:S(2)}) collective-permute-start(bf16[1,256,256]{2,1,0:T(8,128)(2,1)} %bitcast.43), channel_id=1, source_target_pairs={{0,2},{1,3},{2,0},{3,1},{4,6},{5,7},{6,4},{7,5}} | collective-permute-start | bytes 393224 | tf_op jit(solution)/shard_map/ppermute | solution.py:47
  18.8 39.9 %collective-permute-start.6 = (bf16[1,256,256]{2,1,0:T(8,128)(2,1)}, bf16[1,256,256]{2,1,0:T(8,128)(2,1)}, u32[]{:S(2)}, u32[]{:S(2)}) collective-permute-start(bf16[1,256,256]{2,1,0:T(8,128)(2,1)} %bitcast.42), channel_id=1, source_target_pairs={{0,3},{1,2},{2,1},{3,0},{4,7},{5,6},{6,5},{7,4}} | collective-permute-start | bytes 393224 | tf_op jit(solution)/shard_map/ppermute | solution.py:47
  20.5 39.2 %collective-permute-start.7 = (bf16[1,256,256]{2,1,0:T(8,128)(2,1)}, bf16[1,256,256]{2,1,0:T(8,128)(2,1)}, u32[]{:S(2)}, u32[]{:S(2)}) collective-permute-start(bf16[1,256,256]{2,1,0:T(8,128)(2,1)} %bitcast.41), channel_id=1, source_target_pairs={{0,4},{1,5},{2,6},{3,7},{4,0},{5,1},{6,2},{7,3}} | collective-permute-start | bytes 393224 | tf_op jit(solution)/shard_map/ppermute | solution.py:47
  23.9 36.7 %collective-permute-start.8 = (bf16[1,256,256]{2,1,0:T(8,128)(2,1)}, bf16[1,256,256]{2,1,0:T(8,128)(2,1)}, u32[]{:S(2)}, u32[]{:S(2)}) collective-permute-start(bf16[1,256,256]{2,1,0:T(8,128)(2,1)} %bitcast.40), channel_id=1, source_target_pairs={{0,5},{1,4},{2,7},{3,6},{4,1},{5,0},{6,3},{7,2}} | collective-permute-start | bytes 393224 | tf_op jit(solution)/shard_map/ppermute | solution.py:47
  30.6 23.4 %copy-start.5 = (bf16[256,1,256]{0,2,1:T(8,128)(2,1)S(1)}, bf16[256,1,256]{0,2,1:T(8,128)(2,1)}, u32[]{:S(2)}) copy-start(bf16[256,1,256]{0,2,1:T(8,128)(2,1)} %get-tuple-element.6) | copy-start | bytes 393220
  54.0 7.9 %copy-start.7 = (pred[64,512]{1,0:T(8,128)(4,1)S(1)}, pred[64,512]{1,0:T(8,128)(4,1)}, u32[]{:S(2)}) copy-start(pred[64,512]{1,0:T(8,128)(4,1)} %get-tuple-element.23) | copy-start | bytes 98308
  54.3 7.3 %collective-permute-start.9 = (bf16[1,256,256]{2,1,0:T(8,128)(2,1)S(1)}, bf16[1,256,256]{2,1,0:T(8,128)(2,1)S(1)}, u32[]{:S(2)}, u32[]{:S(2)}) collective-permute-start(bf16[1,256,256]{2,1,0:T(8,128)(2,1)S(1)} %bitcast.46), channel_id=1, source_target_pairs={{0,6},{1,7},{2,4},{3,5},{4,2},{5,3},{6,0},{7,1}} | collective-permute-start | bytes 393224 | tf_op jit(solution)/shard_map/ppermute | solution.py:47
  57.8 26.4 %collective-permute-start.10 = (bf16[1,256,256]{2,1,0:T(8,128)(2,1)S(1)}, bf16[1,256,256]{2,1,0:T(8,128)(2,1)S(1)}, u32[]{:S(2)}, u32[]{:S(2)}) collective-permute-start(bf16[1,256,256]{2,1,0:T(8,128)(2,1)S(1)} %bitcast.45), channel_id=1, source_target_pairs={{0,7},{1,6},{2,5},{3,4},{4,3},{5,2},{6,1},{7,0}} | collective-permute-start | bytes 393224 | tf_op jit(solution)/shard_map/ppermute | solution.py:47
  80.7 9.2 %collective-permute-start = (bf16[64,2048]{1,0:T(8,128)(2,1)S(1)}, bf16[64,2048]{1,0:T(8,128)(2,1)S(1)}, u32[]{:S(2)}, u32[]{:S(2)}) collective-permute-start(bf16[64,2048]{1,0:T(8,128)(2,1)S(1)} %bitcast.37), channel_id=1, source_target_pairs={{0,2},{1,3},{2,0},{3,1},{4,6},{5,7},{6,4},{7,5}} | collective-permute-start | bytes 786440 | tf_op jit(solution)/shard_map/ppermute | solution.py:47
  82.5 13.9 %collective-permute-start.1 = (bf16[64,2048]{1,0:T(8,128)(2,1)S(1)}, bf16[64,2048]{1,0:T(8,128)(2,1)S(1)}, u32[]{:S(2)}, u32[]{:S(2)}) collective-permute-start(bf16[64,2048]{1,0:T(8,128)(2,1)S(1)} %bitcast.38), channel_id=1, source_target_pairs={{0,4},{1,5},{2,6},{3,7},{4,0},{5,1},{6,2},{7,3}} | collective-permute-start | bytes 786440 | tf_op jit(solution)/shard_map/ppermute | solution.py:47
  83.9 12.5 %collective-permute-start.2 = (bf16[64,2048]{1,0:T(8,128)(2,1)S(1)}, bf16[64,2048]{1,0:T(8,128)(2,1)S(1)}, u32[]{:S(2)}, u32[]{:S(2)}) collective-permute-start(bf16[64,2048]{1,0:T(8,128)(2,1)S(1)} %bitcast.39), channel_id=1, source_target_pairs={{0,6},{1,7},{2,4},{3,5},{4,2},{5,3},{6,0},{7,1}} | collective-permute-start | bytes 786440 | tf_op jit(solution)/shard_map/ppermute | solution.py:47
  96.4 0.7 copy-start.3
  96.4 0.8 copy-start.4
  97.3 2.7 %collective-permute-start.3 = (bf16[4,64,2048]{2,1,0:T(8,128)(2,1)S(1)}, bf16[4,64,2048]{2,1,0:T(8,128)(2,1)S(1)}, u32[]{:S(2)}, u32[]{:S(2)}) collective-permute-start(bf16[4,64,2048]{2,1,0:T(8,128)(2,1)S(1)} %pad_maximum_fusion), channel_id=1, source_target_pairs={{0,1},{1,0},{2,3},{3,2},{4,5},{5,4},{6,7},{7,6}} | collective-permute-start | bytes 3145736 | tf_op jit(solution)/shard_map/ppermute | solution.py:47
  100.0 1.6 %copy-start.1 = (bf16[512,2048]{1,0:T(8,128)(2,1)S(1)}, bf16[512,2048]{1,0:T(8,128)(2,1)}, u32[]{:S(2)}) copy-start(bf16[512,2048]{1,0:T(8,128)(2,1)} %param.8) | copy-start | bytes 6291460
  100.9 0.7 copy-start.6

commit v2 on v0

v2 whole, which is shorter than its diff:
```python
import functools

import jax
import jax.numpy as jnp
import numpy as np
from jax import lax
from jax.experimental import pallas as pl
from jax.experimental.pallas import tpu as pltpu
from jax.sharding import PartitionSpec as P

F32, BF16 = jnp.float32, jnp.bfloat16
HBM = pl.BlockSpec(memory_space=pltpu.HBM)
VMEM = pl.BlockSpec(memory_space=pltpu.VMEM)
SMEM = pl.BlockSpec(memory_space=pltpu.SMEM)
LOAD_ROWS = 8
CHUNKS = 2
PATCH = 16
LANES = 128


def mm(a, b):
    return jnp.dot(a, b, preferred_element_type=F32)


def rope(x, cosines, sines):
    half = x.shape[-1] // 2
    x1, x2 = x[:, :half], x[:, half:]
    return jnp.concatenate([x1 * cosines - x2 * sines, x2 * cosines + x1 * sines], axis=-1)


def step_kernel(group, lens_s, lens_v, freq, hid_h, wq_h, wk_h, wv_h, wo_h, k_h, v_h,
                k_o, v_o, kn_o, vn_o, y_o,
                hid, wq, wk, wv, wo, cosr, sinr, qrot, qbuf, qf, of, ob, obuf, wsib, psend, ybuf,
                h_sem, k_sem, v_sem, q_s, q_r, w_s, w_r, o_s, o_r, y_s, y_r):
    rows, seq, dim = k_o.shape
    batch = hid.shape[0]
    heads = group
    me = lax.axis_index('tp')
    chip, core = lax.div(me, 2), lax.rem(me, 2)
    start = me * rows
    own = pl.ds(start, rows)
    crows = rows // CHUNKS
    hrows = crows // 2
    scale = dim ** -0.5

    def remote(src, dst, ss, rs, peer):
        return pltpu.make_async_remote_copy(src_ref=src, dst_ref=dst, send_sem=ss, recv_sem=rs,
                                            device_id={'tp': peer}, device_id_type=pl.DeviceIdType.MESH)

    def other(d):
        return lax.rem(me + d, group)

    def load(src, dst, sem, i):
        part = pl.ds(i * LOAD_ROWS, LOAD_ROWS)
        return pltpu.make_async_copy(src.at[part], dst.at[part], sem.at[i])

    barrier = pltpu.get_barrier_semaphore()
    for d in range(1, group):
        pl.semaphore_signal(barrier, inc=1, device_id={'tp': other(d)}, device_id_type=pl.DeviceIdType.MESH)
    weights = [pltpu.make_async_copy(s, d, h_sem.at[i]) for i, (s, d) in enumerate(
        ((hid_h, hid), (wq_h, wq), (wk_h, wk), (wv_h, wv), (wo_h, wo)))]
    for copy in weights:
        copy.start()
    for i in range(rows // LOAD_ROWS):
        load(k_h, k_o, k_sem, i).start()
        load(v_h, v_o, v_sem, i).start()
    pos = jnp.broadcast_to(lens_v[...].astype(F32), (dim // 2, batch)).T
    angles = pos * freq[...]
    cosr[...] = jnp.cos(angles)
    sinr[...] = jnp.sin(angles)
    weights[0].wait()
    weights[1].wait()
    q = mm(hid[...], wq[...]).astype(BF16).astype(F32)
    qrot[...] = rope(q, cosr[...], sinr[...]).astype(BF16)
    pl.semaphore_wait(barrier, group - 1)

    sends = []
    for d in range(1, group):
        peer = other(d)
        copy = remote(qrot.at[pl.ds(peer * rows, rows)], qbuf.at[me], q_s.at[d], q_r.at[d], peer)
        copy.start()
        sends.append(copy)
    qbuf[me] = qrot[own, :]
    for i in range(2, 5):
        weights[i].wait()
    wcopy = remote(wo, wsib, w_s, w_r, chip * 2 + 1 - core)
    wcopy.start()
    mine = hid[own, :]
    k = mm(mine, wk[...]).astype(BF16).astype(F32)
    kn_o[...] = rope(k, cosr[own, :], sinr[own, :]).astype(BF16).astype(F32)
    vn_o[...] = mm(mine, wv[...]).astype(BF16).astype(F32)
    for copy in sends:
        copy.wait()
    for h in range(heads):
        for lane in range(2):
            qf[lane, pl.ds(h * rows, rows), :] = qbuf[h, :, lane * LANES:(lane + 1) * LANES].astype(F32)

    slot = lax.broadcasted_iota(jnp.int32, (heads, seq), 1)

    def attend(b):
        n = lens_s[start + b]
        q = jnp.concatenate([qf[lane, pl.ds(b, heads, stride=rows), :] for lane in range(2)], axis=-1)
        s = lax.dot_general(q.astype(BF16), k_o[b], (((1,), (1,)), ((), ())), preferred_element_type=F32) * scale
        s_new = jnp.sum(q * kn_o[pl.ds(b, 1), :], axis=-1, keepdims=True) * scale
        s = jnp.where(slot < n, s, -1e30)
        top = jnp.maximum(jnp.max(s, axis=-1, keepdims=True), s_new)
        e, e_new = jnp.exp(s - top), jnp.exp(s_new - top)
        total = jnp.sum(e, axis=-1, keepdims=True) + e_new
        new = e_new.astype(BF16).astype(F32) * vn_o[pl.ds(b, 1), :]
        return (mm(e.astype(BF16), v_o[b]) + new) / total

    ocopies, ycopies = [], []
    for ch in range(CHUNKS):
        def body(it, carry):
            step = ch * (crows // LOAD_ROWS) + it
            load(k_h, k_o, k_sem, step).wait()
            load(v_h, v_o, v_sem, step).wait()
            for u in range(LOAD_ROWS):
                b = it * LOAD_ROWS + u
                o = attend(ch * crows + b)
                for lane in range(2):
                    of[lane, pl.ds(b, heads, stride=crows), :] = o[:, lane * LANES:(lane + 1) * LANES]
            return carry

        lax.fori_loop(0, crows // LOAD_ROWS, body, 0)
        for h in range(heads):
            for half in range(2):
                part = pl.ds(h * crows + half * hrows, hrows)
                ob[ch, half, h] = jnp.concatenate([of[lane, part, :] for lane in range(2)], axis=-1).astype(BF16)
        copies = []
        for d in range(1, group):
            peer = other(d)
            pc, ph = lax.div(peer, 2), lax.rem(peer, 2)
            copy = remote(ob.at[ch, ph, pl.ds(pc * 2, 2)], obuf.at[ch, :, pl.ds(me * hrows, hrows)],
                          o_s.at[ch, d], o_r.at[ch, d], peer)
            copy.start()
            copies.append(copy)
        for p in range(2):
            obuf[ch, p, pl.ds(me * hrows, hrows), :] = ob[ch, core, chip * 2 + p]
        ocopies.append(copies)

    wcopy.wait()
    for ch in range(CHUNKS):
        for copy in ocopies[ch]:
            copy.wait()
        o_own, o_sib = obuf[ch, core], obuf[ch, 1 - core]
        copies = []
        for d in list(range(1, group)) + [0]:
            peer = other(d)
            cols = pl.ds(pl.multiple_of(peer * dim, dim), dim)
            part = (mm(o_own, wo[:, cols]) + mm(o_sib, wsib[:, cols])).astype(BF16)
            if d:
                psend[ch, d] = part
                copy = remote(psend.at[ch, d], ybuf.at[ch, core, chip], y_s.at[ch, d], y_r.at[ch, d], peer)
                copy.start()
                copies.append(copy)
            else:
                ybuf[ch, core, chip] = part
        ycopies.append(copies)
    for ch in range(CHUNKS):
        for copy in ycopies[ch]:
            copy.wait()
        for h in range(2):
            total = ybuf[ch, h, 0].astype(F32)
            for c in range(1, group // 2):
                total = total + ybuf[ch, h, c].astype(F32)
            total = total.astype(BF16)
            for s in range(group):
                y_o[pl.ds(s * rows + ch * crows + h * hrows, hrows), :] = total[s * hrows:(s + 1) * hrows]


def store_kernel(lens_s, k_v, v_v, kn, vn, y_i, k_o, v_o, y_o, pk, pv, k_sem, v_sem, pk_sem, pv_sem):
    rows, seq, dim = k_v.shape
    start = lax.axis_index('tp') * rows
    pairs = ((k_v, k_o, k_sem, kn, pk, pk_sem), (v_v, v_o, v_sem, vn, pv, pv_sem))

    def store(pair, i):
        part = pl.ds(i * LOAD_ROWS, LOAD_ROWS)
        return pltpu.make_async_copy(pair[0].at[part], pair[1].at[part], pair[2].at[i])

    def block(b):
        n = lens_s[start + b]
        return n, pl.multiple_of(lax.div(n, PATCH) * PATCH, PATCH)

    def patch(pair, b):
        return pltpu.make_async_copy(pair[4].at[b], pair[1].at[b, pl.ds(block(b)[1], PATCH)], pair[5].at[b])

    for i in range(rows // LOAD_ROWS):
        for pair in pairs:
            store(pair, i).start()
    y_o[...] = y_i[...]
    slot = lax.broadcasted_iota(jnp.int32, (PATCH, dim), 0)

    def fix(b, carry):
        n, base = block(b)
        for src, _, _, new, out, _ in pairs:
            old = src[b, pl.ds(base, PATCH), :].astype(F32)
            line = jnp.broadcast_to(new[pl.ds(b, 1), :], (PATCH, dim))
            out[b] = jnp.where(slot == n - base, line, old).astype(BF16)
        return carry

    lax.fori_loop(0, rows, fix, 0, unroll=4)

    def send(i, carry):
        for pair in pairs:
            store(pair, i).wait()
            for r in range(LOAD_ROWS):
                patch(pair, i * LOAD_ROWS + r).start()
        return carry

    lax.fori_loop(0, rows // LOAD_ROWS, send, 0)

    def finish(b, carry):
        for pair in pairs:
            patch(pair, b).wait()
        return carry

    lax.fori_loop(0, rows, finish, 0)


def solution(mesh):
    group = mesh.shape['tp']
    cache_spec = P(('dp', 'tp'), None, None)

    def local_step(hidden, w_query, w_key, w_value, w_out, k_cache, v_cache, lengths):
        rows, seq, dim = k_cache.shape
        batch, embed = hidden.shape
        shape = jax.ShapeDtypeStruct
        dma, mib = pltpu.SemaphoreType.DMA, 2 ** 20
        freq = np.float32(10000.0) ** (-(np.arange(dim // 2, dtype=np.float32) * np.float32(2.0)) / np.float32(dim))
        hbm = [pltpu.with_memory_space_constraint(x, pltpu.HBM)
               for x in (hidden, w_query, w_key, w_value, w_out, k_cache, v_cache)]
        steps = rows // LOAD_ROWS
        crows = rows // CHUNKS
        hrows = crows // 2
        held = pltpu.VMEM(k_cache.shape, BF16)
        k_all, v_all, k_new, v_new, y = pl.pallas_call(
            functools.partial(step_kernel, group),
            out_shape=(held, held, shape((rows, dim), F32), shape((rows, dim), F32), shape((batch, dim), BF16)),
            in_specs=[SMEM, VMEM, VMEM] + [HBM] * 7,
            out_specs=[VMEM] * 5,
            scratch_shapes=[
                pltpu.VMEM((batch, embed), BF16), pltpu.VMEM((embed, dim), BF16), pltpu.VMEM((embed, dim), BF16),
                pltpu.VMEM((embed, dim), BF16), pltpu.VMEM(w_out.shape, BF16),
                pltpu.VMEM((batch, dim // 2), F32), pltpu.VMEM((batch, dim // 2), F32), pltpu.VMEM((batch, dim), BF16),
                pltpu.VMEM((group, rows, dim), BF16), pltpu.VMEM((2, group * rows, LANES), F32),
                pltpu.VMEM((2, group * crows, LANES), F32), pltpu.VMEM((CHUNKS, 2, group, hrows, dim), BF16),
                pltpu.VMEM((CHUNKS, 2, group * hrows, dim), BF16), pltpu.VMEM(w_out.shape, BF16),
                pltpu.VMEM((CHUNKS, group, group * hrows, dim), BF16),
                pltpu.VMEM((CHUNKS, 2, group // 2, group * hrows, dim), BF16),
                dma((5,)), dma((steps,)), dma((steps,)), dma((group,)), dma((group,)), dma, dma,
                dma((CHUNKS, group)), dma((CHUNKS, group)), dma((CHUNKS, group)), dma((CHUNKS, group)),
            ],
            compiler_params=pltpu.CompilerParams(collective_id=0, has_side_effects=True, vmem_limit_bytes=14 * mib),
        )(lengths, lengths.reshape(1, batch), jnp.asarray(freq).reshape(1, dim // 2), *hbm)
        k_all, v_all = (pltpu.with_memory_space_constraint(x, pltpu.VMEM) for x in (k_all, v_all))
        k_out, v_out, y = pl.pallas_call(
            store_kernel,
            out_shape=(shape(k_cache.shape, BF16), shape(k_cache.shape, BF16), shape((batch, dim), BF16)),
            in_specs=[SMEM] + [VMEM] * 5,
            out_specs=[HBM, HBM, VMEM],
            scratch_shapes=[pltpu.VMEM((rows, PATCH, dim), BF16), pltpu.VMEM((rows, PATCH, dim), BF16),
                            dma((steps,)), dma((steps,)), dma((rows,)), dma((rows,))],
            compiler_params=pltpu.CompilerParams(vmem_limit_bytes=4 * mib),
        )(lengths, k_all, v_all, k_new, v_new, y)
        return y, k_out, v_out

    return jax.shard_map(
        local_step,
        mesh=mesh,
        in_specs=(P('dp', None), P(None, 'tp'), P(), P(), P('tp', None), cache_spec, cache_spec, P('dp')),
        out_specs=(P('dp', 'tp'), cache_spec, cache_spec),
        check_vma=False,
    )
```

time: 113 us -> 67.3 us (0.60)
  Pallas kernels: 0 us -> 65.2 us
  waiting for transfers between devices: 31.8 us -> 0 us
  matrix products: 26.3 us -> 0 us
  other arithmetic: 24.7 us -> 0 us
  between operations: 14.1 us -> 0.65 us
  blocking collectives: 9.58 us -> 0 us
  starting transfers between devices: 4.34 us -> 0 us
    pallas_call x0 -> x2, Pallas kernels: none -> 65.2 us  [the longest x1 51.1 us: local_step(): pl.pallas_call(functools.partial(step_kernel, group), out_shape=(held, he...]
    reduce_scatter x1 -> x0, waiting for transfers between devices: 31.8 us -> none  [local_step(): y_local = lax.psum_scatter(y_part, 'tp', scatter_dimension=1, tiled=True)]
    dot_general x6 -> x0, matrix products: 26.3 us -> none  [the longest x1 10.3 us: attend(): jnp.einsum('bhd,bsd->bhs', q_rot, k_all, preferred_element_type=jnp.float32)]
    select_n x1 -> x0, other arithmetic: 23.1 us -> none  [local_step(): k_out = jnp.where(new_slot, k_rot[:, None, :], k_cache)]
    all_to_all x1 -> x0, blocking collectives: 9.58 us -> none  [local_step(): lax.all_to_all(attn_out.reshape(rows_dev, num_heads * head_dim), 'tp', 1,...]
    all_to_all x1 -> x0, starting transfers between devices: 4.31 us -> none  [local_step(): q_rows = lax.all_to_all(q_cols, 'tp', 0, 1, tiled=True)]
  transfers between devices with their start and end apart: 2 -> 0, of which waited for: 1 -> 0; matrix products, arithmetic and copies ran while one was open for 24% -> 0% of each run, Pallas kernels for 0% -> 0%
where the time goes in v2:
time: 67.3 us; the launch traced here: 67.2 us
  Pallas kernels  65.2 us (97%)
  local copies, waits for them, and re-layouts  1.33 us (2%)
    pallas_call x1, Pallas kernels, local_step(): pl.pallas_call(functools.partial(step_kernel, group), out_shape=(held, he...  51.1 us
    pallas_call x1, Pallas kernels, local_step(): pl.pallas_call(store_kernel, out_shape=(shape(k_cache.shape, BF16), shape...  14.1 us

profile of v2, /device:TPU:0, one launch (start us, length us, event | category | flops | bytes accessed | tf_op | source)
XLA Modules:
  0.0 67.2 jit_solution(17420435855559494075)
XLA Ops:
  0.6 0.0 copy-start
  0.6 0.7 %copy-done = s32[512]{0:T(512)S(1)} copy-done((s32[512]{0:T(512)S(1)}, s32[512]{0:T(512)}, u32[]{:S(2)}) %copy-start) | copy-done | bytes 2072
  1.3 0.0 copy-start.1
  1.3 0.7 copy-done.1
  2.0 51.1 %shard_map.112 = (bf16[64,512,256]{2,1,0:T(8,128)(2,1)S(1)}, bf16[64,512,256]{2,1,0:T(8,128)(2,1)S(1)}, f32[64,256]{1,0:T(8,128)S(1)}, f32[64,256]{1,0:T(8,128)S(1)}, bf16[512,256]{1,0:T(8,128)(2,1)S(1)}) custom-call(s32[512]{0:T(512)S(1)} %copy-done, s32[1,512]{1,0:T(1,128)S(1)} %bitcast.1, f32[1,128]{1,0:T(1,128)S(1)} %copy-done.1, ...), custom_call_target="tpu_custom_call" | custom-call | tf_op jit(solution)/shard_map/pallas_call | solution.py:237
  53.1 14.1 %shard_map.113 = (bf16[64,512,256]{2,1,0:T(8,128)(2,1)}, bf16[64,512,256]{2,1,0:T(8,128)(2,1)}, bf16[512,256]{1,0:T(8,128)(2,1)}) custom-call(s32[512]{0:T(512)S(1)} %copy-done, bf16[64,512,256]{2,1,0:T(8,128)(2,1)S(1)} %get-tuple-element.11.k_v, bf16[64,512,256]{2,1,0:T(8,128)(2,1)S(1)} %get-tuple-element.12.v_v, f32[64,256]{1,0:T(8,128)S(1)} %get-tuple-element.13.kn, ...), custom_call_target="tpu_custom_call" | custom-call | tf_op jit(solution)/shard_map/pallas_call | solution.py:257
Async XLA Ops:
  0.6 0.7 %copy-start = (s32[512]{0:T(512)S(1)}, s32[512]{0:T(512)}, u32[]{:S(2)}) copy-start(s32[512]{0:T(512)} %lens_s.3) | copy-start | bytes 6148
  1.3 0.7 copy-start.1

commit v3 on v2

v3 whole, which is shorter than its diff:
```python
import functools
import math

import jax
import jax.numpy as jnp
from jax import lax
from jax.experimental import pallas as pl
from jax.experimental.pallas import tpu as pltpu
from jax.sharding import PartitionSpec as P

F32, BF16 = jnp.float32, jnp.bfloat16
HBM = pl.BlockSpec(memory_space=pltpu.HBM)
VMEM = pl.BlockSpec(memory_space=pltpu.VMEM)
LOAD_ROWS = 8
CHUNKS = 4
EARLY = 4
PATCH = 16
LANES = 128


def mm(a, b):
    return jnp.dot(a, b, preferred_element_type=F32)


def rope(x, cosines, sines):
    half = x.shape[-1] // 2
    x1, x2 = x[:, :half], x[:, half:]
    return jnp.concatenate([x1 * cosines - x2 * sines, x2 * cosines + x1 * sines], axis=-1)


def step_kernel(group, lens_h, hid_h, wq_h, wk_h, wv_h, wo_h, k_h, v_h,
                k_o, v_o, kn_o, vn_o, y_o,
                lens_s, lens_v, hid, wq, wk, wv, wo, cosr, sinr, qrot, qbuf, qf, of, ob, obuf, wsib, psend, ybuf, yf,
                h_sem, k_sem, v_sem, q_s, q_r, w_s, w_r, o_s, o_r, y_s, y_r):
    rows, seq, dim = k_o.shape
    batch = hid.shape[0]
    heads = group
    me = lax.axis_index('tp')
    chip, core = lax.div(me, 2), lax.rem(me, 2)
    start = me * rows
    own = pl.ds(start, rows)
    crows = rows // CHUNKS
    hrows = crows // 2
    scale = dim ** -0.5

    def remote(src, dst, ss, rs, peer):
        return pltpu.make_async_remote_copy(src_ref=src, dst_ref=dst, send_sem=ss, recv_sem=rs,
                                            device_id={'tp': peer}, device_id_type=pl.DeviceIdType.MESH)

    def other(d):
        return lax.rem(me + d, group)

    def load(src, dst, sem, i):
        part = pl.ds(i * LOAD_ROWS, LOAD_ROWS)
        return pltpu.make_async_copy(src.at[part], dst.at[part], sem.at[i])

    barrier = pltpu.get_barrier_semaphore()
    for d in range(1, group):
        pl.semaphore_signal(barrier, inc=1, device_id={'tp': other(d)}, device_id_type=pl.DeviceIdType.MESH)
    first = [pltpu.make_async_copy(s, d, h_sem.at[i]) for i, (s, d) in enumerate(
        ((hid_h, hid), (wq_h, wq), (lens_h, lens_v), (lens_h.at[0], lens_s)))]
    later = [pltpu.make_async_copy(s, d, h_sem.at[4 + i]) for i, (s, d) in enumerate(
        ((wk_h, wk), (wv_h, wv), (wo_h, wo)))]
    for copy in first:
        copy.start()
    first[2].wait()
    first[3].wait()
    pos = jnp.broadcast_to(lens_v[...].astype(F32), (dim // 2, batch)).T
    freq = jnp.exp(lax.broadcasted_iota(jnp.int32, (1, dim // 2), 1).astype(F32) * (-2.0 * math.log(10000.0) / dim))
    angles = pos * freq
    cosr[...] = jnp.cos(angles)
    sinr[...] = jnp.sin(angles)
    first[0].wait()
    first[1].wait()
    for copy in later:
        copy.start()
    for i in range(EARLY):
        load(k_h, k_o, k_sem, i).start()
        load(v_h, v_o, v_sem, i).start()
    q = mm(hid[...], wq[...]).astype(BF16).astype(F32)
    qrot[...] = rope(q, cosr[...], sinr[...]).astype(BF16)
    pl.semaphore_wait(barrier, group - 1)

    sends = []
    for d in range(1, group):
        peer = other(d)
        copy = remote(qrot.at[pl.ds(peer * rows, rows)], qbuf.at[me], q_s.at[d], q_r.at[d], peer)
        copy.start()
        sends.append(copy)
    qbuf[me] = qrot[own, :]
    for copy in later:
        copy.wait()
    wcopy = remote(wo, wsib, w_s, w_r, chip * 2 + 1 - core)
    wcopy.start()
    mine = hid[own, :]
    k = mm(mine, wk[...]).astype(BF16).astype(F32)
    kn_o[...] = rope(k, cosr[own, :], sinr[own, :]).astype(BF16).astype(F32)
    vn_o[...] = mm(mine, wv[...]).astype(BF16).astype(F32)
    for copy in sends:
        copy.wait()
    for i in range(EARLY, rows // LOAD_ROWS):
        load(k_h, k_o, k_sem, i).start()
        load(v_h, v_o, v_sem, i).start()
    for h in range(heads):
        for lane in range(2):
            qf[lane, pl.ds(h * rows, rows), :] = qbuf[h, :, lane * LANES:(lane + 1) * LANES].astype(F32)

    slot = lax.broadcasted_iota(jnp.int32, (heads, seq), 1)

    def attend(b):
        n = lens_s[start + b]
        q = jnp.concatenate([qf[lane, pl.ds(b, heads, stride=rows), :] for lane in range(2)], axis=-1)
        s = lax.dot_general(q.astype(BF16), k_o[b], (((1,), (1,)), ((), ())), preferred_element_type=F32) * scale
        s_new = jnp.sum(q * kn_o[pl.ds(b, 1), :], axis=-1, keepdims=True) * scale
        s = jnp.where(slot < n, s, -1e30)
        top = jnp.maximum(jnp.max(s, axis=-1, keepdims=True), s_new)
        e, e_new = jnp.exp(s - top), jnp.exp(s_new - top)
        total = jnp.sum(e, axis=-1, keepdims=True) + e_new
        new = e_new.astype(BF16).astype(F32) * vn_o[pl.ds(b, 1), :]
        return (mm(e.astype(BF16), v_o[b]) + new) / total

    ocopies, ycopies = [], []

    def attend_chunk(ch):
        def body(it, carry):
            step = ch * (crows // LOAD_ROWS) + it
            load(k_h, k_o, k_sem, step).wait()
            load(v_h, v_o, v_sem, step).wait()
            for u in range(LOAD_ROWS):
                b = it * LOAD_ROWS + u
                o = attend(ch * crows + b)
                for lane in range(2):
                    of[lane, pl.ds(b, heads, stride=crows), :] = o[:, lane * LANES:(lane + 1) * LANES]
            return carry

        lax.fori_loop(0, crows // LOAD_ROWS, body, 0)
        for h in range(heads):
            for half in range(2):
                part = pl.ds(h * crows + half * hrows, hrows)
                ob[ch, half, h] = jnp.concatenate([of[lane, part, :] for lane in range(2)], axis=-1).astype(BF16)
        copies = []
        for d in range(1, group):
            peer = other(d)
            pc, ph = lax.div(peer, 2), lax.rem(peer, 2)
            copy = remote(ob.at[ch, ph, pl.ds(pc * 2, 2)], obuf.at[ch, :, me], o_s.at[ch, d], o_r.at[ch, d], peer)
            copy.start()
            copies.append(copy)
        for p in range(2):
            obuf[ch, p, me] = ob[ch, core, chip * 2 + p]
        ocopies.append(copies)

    def project_chunk(ch):
        for copy in ocopies[ch]:
            copy.wait()
        o_own, o_sib = (obuf[ch, p].astype(F32).reshape(heads * hrows, dim).astype(BF16) for p in (core, 1 - core))
        copies = []
        for d in list(range(1, group)) + [0]:
            peer = other(d)
            cols = pl.ds(pl.multiple_of(peer * dim, dim), dim)
            part = (mm(o_own, wo[:, cols]) + mm(o_sib, wsib[:, cols])).astype(BF16)
            if d:
                psend[ch, d] = part
                copy = remote(psend.at[ch, d], ybuf.at[ch, core, chip], y_s.at[ch, d], y_r.at[ch, d], peer)
                copy.start()
                copies.append(copy)
            else:
                ybuf[ch, core, chip] = part
        ycopies.append(copies)

    def sum_chunk(ch):
        for copy in ycopies[ch]:
            copy.wait()
        for h in range(2):
            total = ybuf[ch, h, 0].astype(F32)
            for c in range(1, group // 2):
                total = total + ybuf[ch, h, c].astype(F32)
            for s in range(group):
                yf[pl.ds(s * rows + ch * crows + h * hrows, hrows), :] = total[s * hrows:(s + 1) * hrows]

    for ch in range(CHUNKS):
        attend_chunk(ch)
        if ch == 0:
            wcopy.wait()
        else:
            project_chunk(ch - 1)
    project_chunk(CHUNKS - 1)
    for ch in range(CHUNKS):
        sum_chunk(ch)
    y_o[...] = yf[...].astype(BF16)


def store_kernel(lens_h, k_i, v_i, kn, vn, y_i, k_o, v_o, y_o, k_v, v_v, lens_s, l_sem, k_sem, v_sem):
    rows, seq, dim = k_v.shape
    start = lax.axis_index('tp') * rows
    pairs = ((k_v, k_o, k_sem, kn), (v_v, v_o, v_sem, vn))

    def store(pair, i):
        part = pl.ds(i * LOAD_ROWS, LOAD_ROWS)
        return pltpu.make_async_copy(pair[0].at[part], pair[1].at[part], pair[2].at[i])

    lens = pltpu.make_async_copy(lens_h.at[0], lens_s, l_sem)
    lens.start()
    y_o[...] = y_i[...]
    slot = lax.broadcasted_iota(jnp.int32, (PATCH, dim), 0)
    lens.wait()

    def send(i, carry):
        for pair in pairs:
            ref, new = pair[0], pair[3]
            for r in range(LOAD_ROWS):
                b = i * LOAD_ROWS + r
                n = lens_s[start + b]
                base = pl.multiple_of(lax.div(n, PATCH) * PATCH, PATCH)
                line = jnp.broadcast_to(new[pl.ds(b, 1), :], (PATCH, dim))
                old = ref[b, pl.ds(base, PATCH), :].astype(F32)
                ref[b, pl.ds(base, PATCH), :] = jnp.where(slot == n - base, line, old).astype(BF16)
            store(pair, i).start()
        return carry

    lax.fori_loop(0, rows // LOAD_ROWS, send, 0)
    for i in range(rows // LOAD_ROWS):
        for pair in pairs:
            store(pair, i).wait()


def solution(mesh):
    group = mesh.shape['tp']
    cache_spec = P(('dp', 'tp'), None, None)

    def local_step(hidden, w_query, w_key, w_value, w_out, k_cache, v_cache, lengths):
        rows, seq, dim = k_cache.shape
        batch, embed = hidden.shape
        shape = jax.ShapeDtypeStruct
        dma, mib = pltpu.SemaphoreType.DMA, 2 ** 20
        hbm = [pltpu.with_memory_space_constraint(x, pltpu.HBM)
               for x in (lengths.reshape(1, batch), hidden, w_query, w_key, w_value, w_out, k_cache, v_cache)]
        steps = rows // LOAD_ROWS
        crows = rows // CHUNKS
        hrows = crows // 2
        held = pltpu.VMEM(k_cache.shape, BF16)
        k_all, v_all, k_new, v_new, y = pl.pallas_call(
            functools.partial(step_kernel, group),
            out_shape=(held, held, shape((rows, dim), F32), shape((rows, dim), F32), shape((batch, dim), BF16)),
            in_specs=[HBM] * 8,
            out_specs=[VMEM] * 5,
            scratch_shapes=[
                pltpu.SMEM((batch,), jnp.int32), pltpu.VMEM((1, batch), jnp.int32),
                pltpu.VMEM((batch, embed), BF16), pltpu.VMEM((embed, dim), BF16), pltpu.VMEM((embed, dim), BF16),
                pltpu.VMEM((embed, dim), BF16), pltpu.VMEM(w_out.shape, BF16),
                pltpu.VMEM((batch, dim // 2), F32), pltpu.VMEM((batch, dim // 2), F32), pltpu.VMEM((batch, dim), BF16),
                pltpu.VMEM((group, rows, dim), BF16), pltpu.VMEM((2, group * rows, LANES), F32),
                pltpu.VMEM((2, group * crows, LANES), F32), pltpu.VMEM((CHUNKS, 2, group, hrows, dim), BF16),
                pltpu.VMEM((CHUNKS, 2, group, hrows, dim), BF16), pltpu.VMEM(w_out.shape, BF16),
                pltpu.VMEM((CHUNKS, group, group * hrows, dim), BF16),
                pltpu.VMEM((CHUNKS, 2, group // 2, group * hrows, dim), BF16), pltpu.VMEM((batch, dim), F32),
                dma((7,)), dma((steps,)), dma((steps,)), dma((group,)), dma((group,)), dma, dma,
                dma((CHUNKS, group)), dma((CHUNKS, group)), dma((CHUNKS, group)), dma((CHUNKS, group)),
            ],
            compiler_params=pltpu.CompilerParams(collective_id=0, has_side_effects=True, vmem_limit_bytes=14 * mib),
        )(*hbm)
        k_all, v_all = (pltpu.with_memory_space_constraint(x, pltpu.VMEM) for x in (k_all, v_all))
        k_out, v_out, y, _, _ = pl.pallas_call(
            store_kernel,
            out_shape=(shape(k_cache.shape, BF16), shape(k_cache.shape, BF16), shape((batch, dim), BF16), held, held),
            in_specs=[HBM] + [VMEM] * 5,
            out_specs=[HBM, HBM, VMEM, VMEM, VMEM],
            input_output_aliases={1: 3, 2: 4},
            scratch_shapes=[pltpu.SMEM((batch,), jnp.int32), dma, dma((steps,)), dma((steps,))],
            compiler_params=pltpu.CompilerParams(vmem_limit_bytes=4 * mib),
        )(hbm[0], k_all, v_all, k_new, v_new, y)
        return y, k_out, v_out

    return jax.shard_map(
        local_step,
        mesh=mesh,
        in_specs=(P('dp', None), P(None, 'tp'), P(), P(), P('tp', None), cache_spec, cache_spec, P('dp')),
        out_specs=(P('dp', 'tp'), cache_spec, cache_spec),
        check_vma=False,
    )
```

time: 67.3 us -> 58.6 us (0.87)
  Pallas kernels: 65.2 us -> 57.8 us
  local copies, waits for them, and re-layouts: 1.33 us -> 0 us
    pallas_call x1, Pallas kernels: 51.1 us -> 45.3 us  [local_step(): pl.pallas_call(functools.partial(step_kernel, group), out_shape=(held, he...]
    pallas_call x1, Pallas kernels: 14.1 us -> 12.5 us  [local_step(): pl.pallas_call(store_kernel, out_shape=(shape(k_cache.shape, BF16), shape...]
    unnamed x4 -> x0, local copies, waits for them, and re-layouts: 1.33 us -> none
where the time goes in v3:
time: 58.6 us; the launch traced here: 58.5 us
  Pallas kernels  57.8 us (99%)
  between operations  0.64 us (1%)
    pallas_call x1, Pallas kernels, local_step(): pl.pallas_call(functools.partial(step_kernel, group), out_shape=(held, he...  45.3 us
    pallas_call x1, Pallas kernels, local_step(): pl.pallas_call(store_kernel, out_shape=(shape(k_cache.shape, BF16), shape...  12.5 us

profile of v3, /device:TPU:0, one launch (start us, length us, event | category | flops | bytes accessed | tf_op | source)
XLA Modules:
  0.0 58.5 jit_solution(7969153614747028212)
XLA Ops:
  0.6 45.3 %shard_map.103 = (bf16[64,512,256]{2,1,0:T(8,128)(2,1)S(1)}, bf16[64,512,256]{2,1,0:T(8,128)(2,1)S(1)}, f32[64,256]{1,0:T(8,128)S(1)}, f32[64,256]{1,0:T(8,128)S(1)}, bf16[512,256]{1,0:T(8,128)(2,1)S(1)}) custom-call(s32[1,512]{1,0:T(1,128)} %bitcast.1, bf16[512,2048]{1,0:T(8,128)(2,1)} %hid_h.1, bf16[2048,256]{1,0:T(8,128)(2,1)} %wq_h.1, ...), custom_call_target="tpu_custom_call" | custom-call | tf_op jit(solution)/shard_map/pallas_call | solution.py:241
  46.0 12.5 %shard_map.104 = (bf16[64,512,256]{2,1,0:T(8,128)(2,1)}, bf16[64,512,256]{2,1,0:T(8,128)(2,1)}, bf16[512,256]{1,0:T(8,128)(2,1)}, bf16[64,512,256]{2,1,0:T(8,128)(2,1)S(1)}, bf16[64,512,256]{2,1,0:T(8,128)(2,1)S(1)}) custom-call(s32[1,512]{1,0:T(1,128)} %bitcast.2, ...), custom_call_target="tpu_custom_call", output_to_operand_aliasing={{3}: (1, {}), {4}: (2, {})} | custom-call | tf_op jit(solution)/shard_map/pallas_call | solution.py:262

commit v4 on v3

--- a/solution.py
+++ b/solution.py
@@ -12,7 +12,7 @@
 HBM = pl.BlockSpec(memory_space=pltpu.HBM)
 VMEM = pl.BlockSpec(memory_space=pltpu.VMEM)
 LOAD_ROWS = 8
-CHUNKS = 4
+CHUNKS = 2
 EARLY = 4
 PATCH = 16
 LANES = 128
@@ -61,7 +61,7 @@
         ((hid_h, hid), (wq_h, wq), (lens_h, lens_v), (lens_h.at[0], lens_s)))]
     later = [pltpu.make_async_copy(s, d, h_sem.at[4 + i]) for i, (s, d) in enumerate(
         ((wk_h, wk), (wv_h, wv), (wo_h, wo)))]
-    for copy in first:
+    for copy in first + later:
         copy.start()
     first[2].wait()
     first[3].wait()
@@ -72,8 +72,6 @@
     sinr[...] = jnp.sin(angles)
     first[0].wait()
     first[1].wait()
-    for copy in later:
-        copy.start()
     for i in range(EARLY):
         load(k_h, k_o, k_sem, i).start()
         load(v_h, v_o, v_sem, i).start()

time: 58.6 us -> 59.6 us (1.017)
  Pallas kernels: 57.8 us -> 58.8 us
    pallas_call x1, Pallas kernels: 45.3 us -> 46.3 us  [local_step(): pl.pallas_call(functools.partial(step_kernel, group), out_shape=(held, he...]
where the time goes in v4:
time: 59.6 us; the launch traced here: 59.5 us
  Pallas kernels  58.8 us (99%)
  between operations  0.64 us (1%)
    pallas_call x1, Pallas kernels, local_step(): pl.pallas_call(functools.partial(step_kernel, group), out_shape=(held, he...  46.3 us
    pallas_call x1, Pallas kernels, local_step(): pl.pallas_call(store_kernel, out_shape=(shape(k_cache.shape, BF16), shape...  12.5 us

profile of v4, /device:TPU:0, one launch (start us, length us, event | category | flops | bytes accessed | tf_op | source)
XLA Modules:
  0.0 59.5 jit_solution(6280856495067493101)
XLA Ops:
  0.6 46.3 %shard_map.103 = (bf16[64,512,256]{2,1,0:T(8,128)(2,1)S(1)}, bf16[64,512,256]{2,1,0:T(8,128)(2,1)S(1)}, f32[64,256]{1,0:T(8,128)S(1)}, f32[64,256]{1,0:T(8,128)S(1)}, bf16[512,256]{1,0:T(8,128)(2,1)S(1)}) custom-call(s32[1,512]{1,0:T(1,128)} %bitcast.1, bf16[512,2048]{1,0:T(8,128)(2,1)} %hid_h.1, bf16[2048,256]{1,0:T(8,128)(2,1)} %wq_h.1, ...), custom_call_target="tpu_custom_call" | custom-call | tf_op jit(solution)/shard_map/pallas_call | solution.py:239
  47.0 12.5 %shard_map.104 = (bf16[64,512,256]{2,1,0:T(8,128)(2,1)}, bf16[64,512,256]{2,1,0:T(8,128)(2,1)}, bf16[512,256]{1,0:T(8,128)(2,1)}, bf16[64,512,256]{2,1,0:T(8,128)(2,1)S(1)}, bf16[64,512,256]{2,1,0:T(8,128)(2,1)S(1)}) custom-call(s32[1,512]{1,0:T(1,128)} %bitcast.2, ...), custom_call_target="tpu_custom_call", output_to_operand_aliasing={{3}: (1, {}), {4}: (2, {})} | custom-call | tf_op jit(solution)/shard_map/pallas_call | solution.py:260

commit v5 on v4

--- a/solution.py
+++ b/solution.py
@@ -12,10 +12,11 @@
 HBM = pl.BlockSpec(memory_space=pltpu.HBM)
 VMEM = pl.BlockSpec(memory_space=pltpu.VMEM)
 LOAD_ROWS = 8
-CHUNKS = 2
+CHUNKS = 4
 EARLY = 4
 PATCH = 16
 LANES = 128
+GROUP = 4
 
 
 def mm(a, b):
@@ -101,40 +102,46 @@
         load(v_h, v_o, v_sem, i).start()
     for h in range(heads):
         for lane in range(2):
-            qf[lane, pl.ds(h * rows, rows), :] = qbuf[h, :, lane * LANES:(lane + 1) * LANES].astype(F32)
+            qf[lane, pl.ds(h * (rows + 1), rows), :] = qbuf[h, :, lane * LANES:(lane + 1) * LANES].astype(F32)
 
     slot = lax.broadcasted_iota(jnp.int32, (heads, seq), 1)
 
-    def attend(b):
+    def scores(b):
         n = lens_s[start + b]
-        q = jnp.concatenate([qf[lane, pl.ds(b, heads, stride=rows), :] for lane in range(2)], axis=-1)
+        q = jnp.concatenate([qf[lane, pl.ds(b, heads, stride=rows + 1), :] for lane in range(2)], axis=-1)
         s = lax.dot_general(q.astype(BF16), k_o[b], (((1,), (1,)), ((), ())), preferred_element_type=F32) * scale
         s_new = jnp.sum(q * kn_o[pl.ds(b, 1), :], axis=-1, keepdims=True) * scale
-        s = jnp.where(slot < n, s, -1e30)
+        return jnp.where(slot < n, s, -1e30), s_new
+
+    def softmax(s, s_new):
         top = jnp.maximum(jnp.max(s, axis=-1, keepdims=True), s_new)
         e, e_new = jnp.exp(s - top), jnp.exp(s_new - top)
-        total = jnp.sum(e, axis=-1, keepdims=True) + e_new
-        new = e_new.astype(BF16).astype(F32) * vn_o[pl.ds(b, 1), :]
-        return (mm(e.astype(BF16), v_o[b]) + new) / total
+        return e.astype(BF16), e_new.astype(BF16).astype(F32), jnp.sum(e, axis=-1, keepdims=True) + e_new
+
+    def attend(first_row, crow):
+        groups = [range(g, g + GROUP) for g in range(0, crow, GROUP)]
+        ready = None
+        for g in range(len(groups) + 1):
+            nxt = [scores(first_row + u) for u in groups[g]] if g < len(groups) else None
+            if ready is not None:
+                soft = [softmax(*pair) for pair in ready]
+                outs = [mm(e, v_o[first_row + u]) for (e, _, _), u in zip(soft, groups[g - 1])]
+                for o, (_, e_new, total), u in zip(outs, soft, groups[g - 1]):
+                    o = (o + e_new * vn_o[pl.ds(first_row + u, 1), :]) / total
+                    for lane in range(2):
+                        of[lane, pl.ds(u, heads, stride=crow + 1), :] = o[:, lane * LANES:(lane + 1) * LANES]
+            ready = nxt
 
     ocopies, ycopies = [], []
 
     def attend_chunk(ch):
-        def body(it, carry):
-            step = ch * (crows // LOAD_ROWS) + it
+        for step in range(ch * crows // LOAD_ROWS, (ch + 1) * crows // LOAD_ROWS):
             load(k_h, k_o, k_sem, step).wait()
             load(v_h, v_o, v_sem, step).wait()
-            for u in range(LOAD_ROWS):
-                b = it * LOAD_ROWS + u
-                o = attend(ch * crows + b)
-                for lane in range(2):
-                    of[lane, pl.ds(b, heads, stride=crows), :] = o[:, lane * LANES:(lane + 1) * LANES]
-            return carry
-
-        lax.fori_loop(0, crows // LOAD_ROWS, body, 0)
+        attend(ch * crows, crows)
         for h in range(heads):
             for half in range(2):
-                part = pl.ds(h * crows + half * hrows, hrows)
+                part = pl.ds(h * (crows + 1) + half * hrows, hrows)
                 ob[ch, half, h] = jnp.concatenate([of[lane, part, :] for lane in range(2)], axis=-1).astype(BF16)
         copies = []
         for d in range(1, group):
@@ -246,8 +253,8 @@
                 pltpu.VMEM((batch, embed), BF16), pltpu.VMEM((embed, dim), BF16), pltpu.VMEM((embed, dim), BF16),
                 pltpu.VMEM((embed, dim), BF16), pltpu.VMEM(w_out.shape, BF16),
                 pltpu.VMEM((batch, dim // 2), F32), pltpu.VMEM((batch, dim // 2), F32), pltpu.VMEM((batch, dim), BF16),
-                pltpu.VMEM((group, rows, dim), BF16), pltpu.VMEM((2, group * rows, LANES), F32),
-                pltpu.VMEM((2, group * crows, LANES), F32), pltpu.VMEM((CHUNKS, 2, group, hrows, dim), BF16),
+                pltpu.VMEM((group, rows, dim), BF16), pltpu.VMEM((2, group * (rows + 1), LANES), F32),
+                pltpu.VMEM((2, group * (crows + 1), LANES), F32), pltpu.VMEM((CHUNKS, 2, group, hrows, dim), BF16),
                 pltpu.VMEM((CHUNKS, 2, group, hrows, dim), BF16), pltpu.VMEM(w_out.shape, BF16),
                 pltpu.VMEM((CHUNKS, group, group * hrows, dim), BF16),
                 pltpu.VMEM((CHUNKS, 2, group // 2, group * hrows, dim), BF16), pltpu.VMEM((batch, dim), F32),

time: 59.6 us -> 46 us (0.77)
  Pallas kernels: 58.8 us -> 45.2 us
    pallas_call x1, Pallas kernels: 46.3 us -> 32.7 us  [local_step(): pl.pallas_call(functools.partial(step_kernel, group), out_shape=(held, he...]
where the time goes in v5:
time: 46 us; the launch traced here: 45.8 us
  Pallas kernels  45.2 us (98%)
  between operations  0.64 us (1%)
    pallas_call x1, Pallas kernels, local_step(): pl.pallas_call(functools.partial(step_kernel, group), out_shape=(held, he...  32.7 us
    pallas_call x1, Pallas kernels, local_step(): pl.pallas_call(store_kernel, out_shape=(shape(k_cache.shape, BF16), shape...  12.5 us

profile of v5, /device:TPU:0, one launch (start us, length us, event | category | flops | bytes accessed | tf_op | source)
XLA Modules:
  0.0 45.8 jit_solution(1262421632837512852)
XLA Ops:
  0.6 32.7 %shard_map.103 = (bf16[64,512,256]{2,1,0:T(8,128)(2,1)S(1)}, bf16[64,512,256]{2,1,0:T(8,128)(2,1)S(1)}, f32[64,256]{1,0:T(8,128)S(1)}, f32[64,256]{1,0:T(8,128)S(1)}, bf16[512,256]{1,0:T(8,128)(2,1)S(1)}) custom-call(s32[1,512]{1,0:T(1,128)} %bitcast.1, bf16[512,2048]{1,0:T(8,128)(2,1)} %hid_h.1, bf16[2048,256]{1,0:T(8,128)(2,1)} %wq_h.1, ...), custom_call_target="tpu_custom_call" | custom-call | tf_op jit(solution)/shard_map/pallas_call | solution.py:246
  33.3 12.5 %shard_map.104 = (bf16[64,512,256]{2,1,0:T(8,128)(2,1)}, bf16[64,512,256]{2,1,0:T(8,128)(2,1)}, bf16[512,256]{1,0:T(8,128)(2,1)}, bf16[64,512,256]{2,1,0:T(8,128)(2,1)S(1)}, bf16[64,512,256]{2,1,0:T(8,128)(2,1)S(1)}) custom-call(s32[1,512]{1,0:T(1,128)} %bitcast.2, ...), custom_call_target="tpu_custom_call", output_to_operand_aliasing={{3}: (1, {}), {4}: (2, {})} | custom-call | tf_op jit(solution)/shard_map/pallas_call | solution.py:267

commit v6 on v5

--- a/solution.py
+++ b/solution.py
@@ -17,6 +17,7 @@
 PATCH = 16
 LANES = 128
 GROUP = 4
+Q_PARTS = 2
 
 
 def mm(a, b):
@@ -80,12 +81,16 @@
     qrot[...] = rope(q, cosr[...], sinr[...]).astype(BF16)
     pl.semaphore_wait(barrier, group - 1)
 
+    qrows = rows // Q_PARTS
     sends = []
-    for d in range(1, group):
-        peer = other(d)
-        copy = remote(qrot.at[pl.ds(peer * rows, rows)], qbuf.at[me], q_s.at[d], q_r.at[d], peer)
-        copy.start()
-        sends.append(copy)
+    for part in range(Q_PARTS):
+        sends.append([])
+        for d in range(1, group):
+            peer = other(d)
+            copy = remote(qrot.at[pl.ds(peer * rows + part * qrows, qrows)], qbuf.at[me, pl.ds(part * qrows, qrows)],
+                          q_s.at[part, d], q_r.at[part, d], peer)
+            copy.start()
+            sends[-1].append(copy)
     qbuf[me] = qrot[own, :]
     for copy in later:
         copy.wait()
@@ -95,15 +100,19 @@
     k = mm(mine, wk[...]).astype(BF16).astype(F32)
     kn_o[...] = rope(k, cosr[own, :], sinr[own, :]).astype(BF16).astype(F32)
     vn_o[...] = mm(mine, wv[...]).astype(BF16).astype(F32)
-    for copy in sends:
-        copy.wait()
+
+    def take_q(part):
+        for copy in sends[part]:
+            copy.wait()
+        for h in range(heads):
+            for lane in range(2):
+                qf[lane, pl.ds(h * (rows + 1) + part * qrows, qrows), :] = qbuf[
+                    h, pl.ds(part * qrows, qrows), lane * LANES:(lane + 1) * LANES].astype(F32)
+
+    take_q(0)
     for i in range(EARLY, rows // LOAD_ROWS):
         load(k_h, k_o, k_sem, i).start()
         load(v_h, v_o, v_sem, i).start()
-    for h in range(heads):
-        for lane in range(2):
-            qf[lane, pl.ds(h * (rows + 1), rows), :] = qbuf[h, :, lane * LANES:(lane + 1) * LANES].astype(F32)
-
     slot = lax.broadcasted_iota(jnp.int32, (heads, seq), 1)
 
     def scores(b):
@@ -183,6 +192,8 @@
                 yf[pl.ds(s * rows + ch * crows + h * hrows, hrows), :] = total[s * hrows:(s + 1) * hrows]
 
     for ch in range(CHUNKS):
+        if ch and (ch * crows) % qrows == 0:
+            take_q(ch * crows // qrows)
         attend_chunk(ch)
         if ch == 0:
             wcopy.wait()
@@ -194,7 +205,7 @@
     y_o[...] = yf[...].astype(BF16)
 
 
-def store_kernel(lens_h, k_i, v_i, kn, vn, y_i, k_o, v_o, y_o, k_v, v_v, lens_s, l_sem, k_sem, v_sem):
+def store_kernel(lens_h, k_i, v_i, kn, vn, y_i, k_o, v_o, y_o, k_v, v_v, lens_s, l_sem, k_sem, v_sem, p_sem):
     rows, seq, dim = k_v.shape
     start = lax.axis_index('tp') * rows
     pairs = ((k_v, k_o, k_sem, kn), (v_v, v_o, v_sem, vn))
@@ -205,27 +216,46 @@
 
     lens = pltpu.make_async_copy(lens_h.at[0], lens_s, l_sem)
     lens.start()
+    for pair in pairs:
+        store(pair, 0).start()
     y_o[...] = y_i[...]
     slot = lax.broadcasted_iota(jnp.int32, (PATCH, dim), 0)
     lens.wait()
 
+    def block(b):
+        n = lens_s[start + b]
+        base = pl.multiple_of(lax.div(n, PATCH) * PATCH, PATCH)
+        return n - base, pl.ds(base, PATCH)
+
+    def patch(pair, b):
+        at, part = block(b)
+        line = jnp.broadcast_to(pair[3][pl.ds(b, 1), :], (PATCH, dim))
+        old = pair[0][b, part, :].astype(F32)
+        pair[0][b, part, :] = jnp.where(slot == at, line, old).astype(BF16)
+
+    def late(p, b):
+        part = block(b)[1]
+        return pltpu.make_async_copy(pairs[p][0].at[b, part], pairs[p][1].at[b, part], p_sem.at[p, b])
+
     def send(i, carry):
         for pair in pairs:
-            ref, new = pair[0], pair[3]
             for r in range(LOAD_ROWS):
-                b = i * LOAD_ROWS + r
-                n = lens_s[start + b]
-                base = pl.multiple_of(lax.div(n, PATCH) * PATCH, PATCH)
-                line = jnp.broadcast_to(new[pl.ds(b, 1), :], (PATCH, dim))
-                old = ref[b, pl.ds(base, PATCH), :].astype(F32)
-                ref[b, pl.ds(base, PATCH), :] = jnp.where(slot == n - base, line, old).astype(BF16)
+                patch(pair, i * LOAD_ROWS + r)
             store(pair, i).start()
         return carry
 
-    lax.fori_loop(0, rows // LOAD_ROWS, send, 0)
-    for i in range(rows // LOAD_ROWS):
+    lax.fori_loop(1, rows // LOAD_ROWS, send, 0)
+    for p in range(2):
+        store(pairs[p], 0).wait()
+        for b in range(LOAD_ROWS):
+            patch(pairs[p], b)
+            late(p, b).start()
+    for i in range(1, rows // LOAD_ROWS):
         for pair in pairs:
             store(pair, i).wait()
+    for p in range(2):
+        for b in range(LOAD_ROWS):
+            late(p, b).wait()
 
 
 def solution(mesh):
@@ -258,7 +288,7 @@
                 pltpu.VMEM((CHUNKS, 2, group, hrows, dim), BF16), pltpu.VMEM(w_out.shape, BF16),
                 pltpu.VMEM((CHUNKS, group, group * hrows, dim), BF16),
                 pltpu.VMEM((CHUNKS, 2, group // 2, group * hrows, dim), BF16), pltpu.VMEM((batch, dim), F32),
-                dma((7,)), dma((steps,)), dma((steps,)), dma((group,)), dma((group,)), dma, dma,
+                dma((7,)), dma((steps,)), dma((steps,)), dma((Q_PARTS, group)), dma((Q_PARTS, group)), dma, dma,
                 dma((CHUNKS, group)), dma((CHUNKS, group)), dma((CHUNKS, group)), dma((CHUNKS, group)),
             ],
             compiler_params=pltpu.CompilerParams(collective_id=0, has_side_effects=True, vmem_limit_bytes=14 * mib),
@@ -270,7 +300,7 @@
             in_specs=[HBM] + [VMEM] * 5,
             out_specs=[HBM, HBM, VMEM, VMEM, VMEM],
             input_output_aliases={1: 3, 2: 4},
-            scratch_shapes=[pltpu.SMEM((batch,), jnp.int32), dma, dma((steps,)), dma((steps,))],
+            scratch_shapes=[pltpu.SMEM((batch,), jnp.int32), dma, dma((steps,)), dma((steps,)), dma((2, LOAD_ROWS))],
             compiler_params=pltpu.CompilerParams(vmem_limit_bytes=4 * mib),
         )(hbm[0], k_all, v_all, k_new, v_new, y)
         return y, k_out, v_out

time: 46 us -> 45 us (0.978)
  Pallas kernels: 45.2 us -> 44.2 us
    pallas_call x1, Pallas kernels: 12.5 us -> 11.9 us  [local_step(): pl.pallas_call(store_kernel, out_shape=(shape(k_cache.shape, BF16), shape...]
where the time goes in v6:
time: 45 us; the launch traced here: 44.9 us
  Pallas kernels  44.2 us (98%)
  between operations  0.64 us (1%)
    pallas_call x1, Pallas kernels, local_step(): pl.pallas_call(functools.partial(step_kernel, group), out_shape=(held, he...  32.3 us
    pallas_call x1, Pallas kernels, local_step(): pl.pallas_call(store_kernel, out_shape=(shape(k_cache.shape, BF16), shape...  11.9 us

profile of v6, /device:TPU:0, one launch (start us, length us, event | category | flops | bytes accessed | tf_op | source)
XLA Modules:
  0.0 44.9 jit_solution(7044224118726392513)
XLA Ops:
  0.6 32.3 %shard_map.103 = (bf16[64,512,256]{2,1,0:T(8,128)(2,1)S(1)}, bf16[64,512,256]{2,1,0:T(8,128)(2,1)S(1)}, f32[64,256]{1,0:T(8,128)S(1)}, f32[64,256]{1,0:T(8,128)S(1)}, bf16[512,256]{1,0:T(8,128)(2,1)S(1)}) custom-call(s32[1,512]{1,0:T(1,128)} %bitcast.1, bf16[512,2048]{1,0:T(8,128)(2,1)} %hid_h.1, bf16[2048,256]{1,0:T(8,128)(2,1)} %wq_h.1, ...), custom_call_target="tpu_custom_call" | custom-call | tf_op jit(solution)/shard_map/pallas_call | solution.py:276
  33.0 11.9 %shard_map.104 = (bf16[64,512,256]{2,1,0:T(8,128)(2,1)}, bf16[64,512,256]{2,1,0:T(8,128)(2,1)}, bf16[512,256]{1,0:T(8,128)(2,1)}, bf16[64,512,256]{2,1,0:T(8,128)(2,1)S(1)}, bf16[64,512,256]{2,1,0:T(8,128)(2,1)S(1)}) custom-call(s32[1,512]{1,0:T(1,128)} %bitcast.2, ...), custom_call_target="tpu_custom_call", output_to_operand_aliasing={{3}: (1, {}), {4}: (2, {})} | custom-call | tf_op jit(solution)/shard_map/pallas_call | solution.py:297

commit v7 on v6

--- a/solution.py
+++ b/solution.py
@@ -32,8 +32,8 @@
 
 def step_kernel(group, lens_h, hid_h, wq_h, wk_h, wv_h, wo_h, k_h, v_h,
                 k_o, v_o, kn_o, vn_o, y_o,
-                lens_s, lens_v, hid, wq, wk, wv, wo, cosr, sinr, qrot, qbuf, qf, of, ob, obuf, wsib, psend, ybuf, yf,
-                h_sem, k_sem, v_sem, q_s, q_r, w_s, w_r, o_s, o_r, y_s, y_r):
+                lens_s, lens_v, hid, wq, wk, wv, wo, cosr, sinr, qrot, qbuf, qf, of, ob, obuf, wsib, psend, ybuf, rel, yf,
+                h_sem, k_sem, v_sem, q_s, q_r, w_s, w_r, o_s, o_r, y_s, y_r, r_r):
     rows, seq, dim = k_o.shape
     batch = hid.shape[0]
     heads = group
@@ -163,31 +163,56 @@
             obuf[ch, p, me] = ob[ch, core, chip * 2 + p]
         ocopies.append(copies)
 
+    x, y = lax.rem(chip, 2), lax.div(chip, 2)
+
+    def device(dy, dx, k):
+        return (y + dy - 2 * y * dy) * 4 + (x + dx - 2 * x * dx) * 2 + k
+
+    def partial(ch, peer):
+        o_own, o_sib = (obuf[ch, p].astype(F32).reshape(heads * hrows, dim).astype(BF16) for p in (core, 1 - core))
+        cols = pl.ds(pl.multiple_of(peer * dim, dim), dim)
+        return mm(o_own, wo[:, cols]) + mm(o_sib, wsib[:, cols])
+
+    relays = []
+
+    def push(ch, i, value, dst, sem, peer):
+        psend[ch, i] = value.astype(BF16)
+        copy = remote(psend.at[ch, i], dst, y_s.at[ch, i], sem, peer)
+        copy.start()
+        return copy
+
     def project_chunk(ch):
         for copy in ocopies[ch]:
             copy.wait()
-        o_own, o_sib = (obuf[ch, p].astype(F32).reshape(heads * hrows, dim).astype(BF16) for p in (core, 1 - core))
-        copies = []
-        for d in list(range(1, group)) + [0]:
-            peer = other(d)
-            cols = pl.ds(pl.multiple_of(peer * dim, dim), dim)
-            part = (mm(o_own, wo[:, cols]) + mm(o_sib, wsib[:, cols])).astype(BF16)
-            if d:
-                psend[ch, d] = part
-                copy = remote(psend.at[ch, d], ybuf.at[ch, core, chip], y_s.at[ch, d], y_r.at[ch, d], peer)
-                copy.start()
-                copies.append(copy)
-            else:
-                ybuf[ch, core, chip] = part
-        ycopies.append(copies)
+        relays.append([
+            push(ch, 0, partial(ch, device(1, 1, 0)), rel.at[ch, 0], r_r.at[ch, 0], device(0, 1, core)),
+            push(ch, 1, partial(ch, device(1, 1, 1)), rel.at[ch, 1], r_r.at[ch, 1], device(1, 0, core))])
+        ycopies.append([
+            push(ch, 2, partial(ch, device(0, 1, 0)), ybuf.at[ch, core, 1], y_r.at[ch, 1, core], device(0, 1, 0)),
+            push(ch, 3, partial(ch, device(1, 0, 1)), ybuf.at[ch, core, 2], y_r.at[ch, 2, core], device(1, 0, 1)),
+            push(ch, 4, partial(ch, device(0, 0, 1 - core)), ybuf.at[ch, core, 0], y_r.at[ch, 0, core],
+                 device(0, 0, 1 - core))])
+        ybuf[ch, core, 0] = partial(ch, me).astype(BF16)
+
+    def relay_chunk(ch):
+        for i, peer, slot in ((0, device(1, 0, 0), 2), (1, device(0, 1, 1), 1)):
+            mine = partial(ch, peer)
+            relays[ch][i].wait()
+            ycopies[ch].append(push(ch, 5 + i, mine + rel[ch, i].astype(F32), ybuf.at[ch, core, slot],
+                                    y_r.at[ch, slot, core], peer))
 
     def sum_chunk(ch):
+        def arrived(h, part):
+            remote(ybuf.at[ch, h, part], ybuf.at[ch, h, part], y_s.at[ch, 4], y_r.at[ch, part, h], me).wait_recv()
+
         for copy in ycopies[ch]:
-            copy.wait()
+            copy.wait_send()
+        arrived(1 - core, 0)
         for h in range(2):
-            total = ybuf[ch, h, 0].astype(F32)
-            for c in range(1, group // 2):
-                total = total + ybuf[ch, h, c].astype(F32)
+            arrived(h, 1)
+            arrived(h, 2)
+        for h in range(2):
+            total = ybuf[ch, h, 0].astype(F32) + ybuf[ch, h, 1].astype(F32) + ybuf[ch, h, 2].astype(F32)
             for s in range(group):
                 yf[pl.ds(s * rows + ch * crows + h * hrows, hrows), :] = total[s * hrows:(s + 1) * hrows]
 
@@ -199,7 +224,11 @@
             wcopy.wait()
         else:
             project_chunk(ch - 1)
+        if ch > 1:
+            relay_chunk(ch - 2)
     project_chunk(CHUNKS - 1)
+    relay_chunk(CHUNKS - 2)
+    relay_chunk(CHUNKS - 1)
     for ch in range(CHUNKS):
         sum_chunk(ch)
     y_o[...] = yf[...].astype(BF16)
@@ -286,10 +315,11 @@
                 pltpu.VMEM((group, rows, dim), BF16), pltpu.VMEM((2, group * (rows + 1), LANES), F32),
                 pltpu.VMEM((2, group * (crows + 1), LANES), F32), pltpu.VMEM((CHUNKS, 2, group, hrows, dim), BF16),
                 pltpu.VMEM((CHUNKS, 2, group, hrows, dim), BF16), pltpu.VMEM(w_out.shape, BF16),
-                pltpu.VMEM((CHUNKS, group, group * hrows, dim), BF16),
-                pltpu.VMEM((CHUNKS, 2, group // 2, group * hrows, dim), BF16), pltpu.VMEM((batch, dim), F32),
+                pltpu.VMEM((CHUNKS, 7, group * hrows, dim), BF16),
+                pltpu.VMEM((CHUNKS, 2, 3, group * hrows, dim), BF16), pltpu.VMEM((CHUNKS, 2, group * hrows, dim), BF16),
+                pltpu.VMEM((batch, dim), F32),
                 dma((7,)), dma((steps,)), dma((steps,)), dma((Q_PARTS, group)), dma((Q_PARTS, group)), dma, dma,
-                dma((CHUNKS, group)), dma((CHUNKS, group)), dma((CHUNKS, group)), dma((CHUNKS, group)),
+                dma((CHUNKS, group)), dma((CHUNKS, group)), dma((CHUNKS, 7)), dma((CHUNKS, 3, 2)), dma((CHUNKS, 2)),
             ],
             compiler_params=pltpu.CompilerParams(collective_id=0, has_side_effects=True, vmem_limit_bytes=14 * mib),
         )(*hbm)

time: 45 us -> 45.6 us (1.013)
  Pallas kernels: 44.2 us -> 44.8 us
    pallas_call x1, Pallas kernels: 32.3 us -> 32.9 us  [local_step(): pl.pallas_call(functools.partial(step_kernel, group), out_shape=(held, he...]
where the time goes in v7:
time: 45.6 us; the launch traced here: 45.5 us
  Pallas kernels  44.8 us (98%)
  between operations  0.64 us (1%)
    pallas_call x1, Pallas kernels, local_step(): pl.pallas_call(functools.partial(step_kernel, group), out_shape=(held, he...  32.9 us
    pallas_call x1, Pallas kernels, local_step(): pl.pallas_call(store_kernel, out_shape=(shape(k_cache.shape, BF16), shape...  11.9 us

profile of v7, /device:TPU:0, one launch (start us, length us, event | category | flops | bytes accessed | tf_op | source)
XLA Modules:
  0.0 45.5 jit_solution(16127473496361602752)
XLA Ops:
  0.6 32.9 %shard_map.103 = (bf16[64,512,256]{2,1,0:T(8,128)(2,1)S(1)}, bf16[64,512,256]{2,1,0:T(8,128)(2,1)S(1)}, f32[64,256]{1,0:T(8,128)S(1)}, f32[64,256]{1,0:T(8,128)S(1)}, bf16[512,256]{1,0:T(8,128)(2,1)S(1)}) custom-call(s32[1,512]{1,0:T(1,128)} %bitcast.1, bf16[512,2048]{1,0:T(8,128)(2,1)} %hid_h.1, bf16[2048,256]{1,0:T(8,128)(2,1)} %wq_h.1, ...), custom_call_target="tpu_custom_call" | custom-call | tf_op jit(solution)/shard_map/pallas_call | solution.py:305
  33.5 11.9 %shard_map.104 = (bf16[64,512,256]{2,1,0:T(8,128)(2,1)}, bf16[64,512,256]{2,1,0:T(8,128)(2,1)}, bf16[512,256]{1,0:T(8,128)(2,1)}, bf16[64,512,256]{2,1,0:T(8,128)(2,1)S(1)}, bf16[64,512,256]{2,1,0:T(8,128)(2,1)S(1)}) custom-call(s32[1,512]{1,0:T(1,128)} %bitcast.2, ...), custom_call_target="tpu_custom_call", output_to_operand_aliasing={{3}: (1, {}), {4}: (2, {})} | custom-call | tf_op jit(solution)/shard_map/pallas_call | solution.py:327

commit v8 on v6

--- a/solution.py
+++ b/solution.py
@@ -63,10 +63,12 @@
         ((hid_h, hid), (wq_h, wq), (lens_h, lens_v), (lens_h.at[0], lens_s)))]
     later = [pltpu.make_async_copy(s, d, h_sem.at[4 + i]) for i, (s, d) in enumerate(
         ((wk_h, wk), (wv_h, wv), (wo_h, wo)))]
-    for copy in first + later:
+    for copy in first:
         copy.start()
     first[2].wait()
     first[3].wait()
+    for copy in later:
+        copy.start()
     pos = jnp.broadcast_to(lens_v[...].astype(F32), (dim // 2, batch)).T
     freq = jnp.exp(lax.broadcasted_iota(jnp.int32, (1, dim // 2), 1).astype(F32) * (-2.0 * math.log(10000.0) / dim))
     angles = pos * freq
@@ -109,7 +111,9 @@
                 qf[lane, pl.ds(h * (rows + 1) + part * qrows, qrows), :] = qbuf[
                     h, pl.ds(part * qrows, qrows), lane * LANES:(lane + 1) * LANES].astype(F32)
 
-    take_q(0)
+    for i in range(EARLY):
+        load(k_h, k_o, k_sem, i).wait()
+        load(v_h, v_o, v_sem, i).wait()
     for i in range(EARLY, rows // LOAD_ROWS):
         load(k_h, k_o, k_sem, i).start()
         load(v_h, v_o, v_sem, i).start()
@@ -127,27 +131,24 @@
         e, e_new = jnp.exp(s - top), jnp.exp(s_new - top)
         return e.astype(BF16), e_new.astype(BF16).astype(F32), jnp.sum(e, axis=-1, keepdims=True) + e_new
 
-    def attend(first_row, crow):
-        groups = [range(g, g + GROUP) for g in range(0, crow, GROUP)]
-        ready = None
-        for g in range(len(groups) + 1):
-            nxt = [scores(first_row + u) for u in groups[g]] if g < len(groups) else None
-            if ready is not None:
-                soft = [softmax(*pair) for pair in ready]
-                outs = [mm(e, v_o[first_row + u]) for (e, _, _), u in zip(soft, groups[g - 1])]
-                for o, (_, e_new, total), u in zip(outs, soft, groups[g - 1]):
-                    o = (o + e_new * vn_o[pl.ds(first_row + u, 1), :]) / total
-                    for lane in range(2):
-                        of[lane, pl.ds(u, heads, stride=crow + 1), :] = o[:, lane * LANES:(lane + 1) * LANES]
-            ready = nxt
+    def value(b, row, e, e_new, total):
+        o = (mm(e, v_o[b]) + e_new * vn_o[pl.ds(b, 1), :]) / total
+        return row, o
+
+    def keep(row, o):
+        for lane in range(2):
+            of[lane, pl.ds(row, heads, stride=crows + 1), :] = o[:, lane * LANES:(lane + 1) * LANES]
 
     ocopies, ycopies = [], []
 
-    def attend_chunk(ch):
-        for step in range(ch * crows // LOAD_ROWS, (ch + 1) * crows // LOAD_ROWS):
+    def begin_chunk(ch):
+        if (ch * crows) % qrows == 0:
+            take_q(ch * crows // qrows)
+        for step in range(max(EARLY, ch * crows // LOAD_ROWS), (ch + 1) * crows // LOAD_ROWS):
             load(k_h, k_o, k_sem, step).wait()
             load(v_h, v_o, v_sem, step).wait()
-        attend(ch * crows, crows)
+
+    def send_chunk(ch):
         for h in range(heads):
             for half in range(2):
                 part = pl.ds(h * (crows + 1) + half * hrows, hrows)
@@ -191,14 +192,24 @@
             for s in range(group):
                 yf[pl.ds(s * rows + ch * crows + h * hrows, hrows), :] = total[s * hrows:(s + 1) * hrows]
 
-    for ch in range(CHUNKS):
-        if ch and (ch * crows) % qrows == 0:
-            take_q(ch * crows // qrows)
-        attend_chunk(ch)
-        if ch == 0:
-            wcopy.wait()
-        else:
-            project_chunk(ch - 1)
+    per_chunk = crows // GROUP
+    ready = None
+    for g in range(CHUNKS * per_chunk + 1):
+        ch = g // per_chunk
+        if ch < CHUNKS and g % per_chunk == 0:
+            begin_chunk(ch)
+        nxt = [(b, scores(b)) for b in range(g * GROUP, (g + 1) * GROUP)] if ch < CHUNKS else None
+        if ready is not None:
+            soft = [(b, softmax(*pair)) for b, pair in ready]
+            for row, o in [value(b, b % crows, *parts) for b, parts in soft]:
+                keep(row, o)
+            if g % per_chunk == 0:
+                send_chunk(ch - 1)
+                if ch == 1:
+                    wcopy.wait()
+                else:
+                    project_chunk(ch - 2)
+        ready = nxt
     project_chunk(CHUNKS - 1)
     for ch in range(CHUNKS):
         sum_chunk(ch)

time: 45 us -> 46.4 us (1.031)
  Pallas kernels: 44.2 us -> 45.6 us
    pallas_call x1, Pallas kernels: 32.3 us -> 33.7 us  [local_step(): pl.pallas_call(functools.partial(step_kernel, group), out_shape=(held, he...]
where the time goes in v8:
time: 46.4 us; the launch traced here: 46.3 us
  Pallas kernels  45.6 us (98%)
  between operations  0.64 us (1%)
    pallas_call x1, Pallas kernels, local_step(): pl.pallas_call(functools.partial(step_kernel, group), out_shape=(held, he...  33.7 us
    pallas_call x1, Pallas kernels, local_step(): pl.pallas_call(store_kernel, out_shape=(shape(k_cache.shape, BF16), shape...  11.9 us

profile of v8, /device:TPU:0, one launch (start us, length us, event | category | flops | bytes accessed | tf_op | source)
XLA Modules:
  0.0 46.3 jit_solution(3188503189529418040)
XLA Ops:
  0.6 33.7 %shard_map.103 = (bf16[64,512,256]{2,1,0:T(8,128)(2,1)S(1)}, bf16[64,512,256]{2,1,0:T(8,128)(2,1)S(1)}, f32[64,256]{1,0:T(8,128)S(1)}, f32[64,256]{1,0:T(8,128)S(1)}, bf16[512,256]{1,0:T(8,128)(2,1)S(1)}) custom-call(s32[1,512]{1,0:T(1,128)} %bitcast.1, bf16[512,2048]{1,0:T(8,128)(2,1)} %hid_h.1, bf16[2048,256]{1,0:T(8,128)(2,1)} %wq_h.1, ...), custom_call_target="tpu_custom_call" | custom-call | tf_op jit(solution)/shard_map/pallas_call | solution.py:287
  34.3 11.9 %shard_map.104 = (bf16[64,512,256]{2,1,0:T(8,128)(2,1)}, bf16[64,512,256]{2,1,0:T(8,128)(2,1)}, bf16[512,256]{1,0:T(8,128)(2,1)}, bf16[64,512,256]{2,1,0:T(8,128)(2,1)S(1)}, bf16[64,512,256]{2,1,0:T(8,128)(2,1)S(1)}) custom-call(s32[1,512]{1,0:T(1,128)} %bitcast.2, ...), custom_call_target="tpu_custom_call", output_to_operand_aliasing={{3}: (1, {}), {4}: (2, {})} | custom-call | tf_op jit(solution)/shard_map/pallas_call | solution.py:308

commit v9 on v8

--- a/solution.py
+++ b/solution.py
@@ -63,12 +63,10 @@
         ((hid_h, hid), (wq_h, wq), (lens_h, lens_v), (lens_h.at[0], lens_s)))]
     later = [pltpu.make_async_copy(s, d, h_sem.at[4 + i]) for i, (s, d) in enumerate(
         ((wk_h, wk), (wv_h, wv), (wo_h, wo)))]
-    for copy in first:
+    for copy in first + later:
         copy.start()
     first[2].wait()
     first[3].wait()
-    for copy in later:
-        copy.start()
     pos = jnp.broadcast_to(lens_v[...].astype(F32), (dim // 2, batch)).T
     freq = jnp.exp(lax.broadcasted_iota(jnp.int32, (1, dim // 2), 1).astype(F32) * (-2.0 * math.log(10000.0) / dim))
     angles = pos * freq
@@ -111,9 +109,7 @@
                 qf[lane, pl.ds(h * (rows + 1) + part * qrows, qrows), :] = qbuf[
                     h, pl.ds(part * qrows, qrows), lane * LANES:(lane + 1) * LANES].astype(F32)
 
-    for i in range(EARLY):
-        load(k_h, k_o, k_sem, i).wait()
-        load(v_h, v_o, v_sem, i).wait()
+    take_q(0)
     for i in range(EARLY, rows // LOAD_ROWS):
         load(k_h, k_o, k_sem, i).start()
         load(v_h, v_o, v_sem, i).start()
@@ -142,9 +138,9 @@
     ocopies, ycopies = [], []
 
     def begin_chunk(ch):
-        if (ch * crows) % qrows == 0:
+        if ch and (ch * crows) % qrows == 0:
             take_q(ch * crows // qrows)
-        for step in range(max(EARLY, ch * crows // LOAD_ROWS), (ch + 1) * crows // LOAD_ROWS):
+        for step in range(ch * crows // LOAD_ROWS, (ch + 1) * crows // LOAD_ROWS):
             load(k_h, k_o, k_sem, step).wait()
             load(v_h, v_o, v_sem, step).wait()
 
@@ -216,7 +212,7 @@
     y_o[...] = yf[...].astype(BF16)
 
 
-def store_kernel(lens_h, k_i, v_i, kn, vn, y_i, k_o, v_o, y_o, k_v, v_v, lens_s, l_sem, k_sem, v_sem, p_sem):
+def store_kernel(lens_h, k_i, v_i, kn, vn, y_i, k_o, v_o, y_o, k_v, v_v, lens_s, l_sem, y_sem, k_sem, v_sem, p_sem):
     rows, seq, dim = k_v.shape
     start = lax.axis_index('tp') * rows
     pairs = ((k_v, k_o, k_sem, kn), (v_v, v_o, v_sem, vn))
@@ -229,7 +225,8 @@
     lens.start()
     for pair in pairs:
         store(pair, 0).start()
-    y_o[...] = y_i[...]
+    y_copy = pltpu.make_async_copy(y_i, y_o, y_sem)
+    y_copy.start()
     slot = lax.broadcasted_iota(jnp.int32, (PATCH, dim), 0)
     lens.wait()
 
@@ -267,6 +264,7 @@
     for p in range(2):
         for b in range(LOAD_ROWS):
             late(p, b).wait()
+    y_copy.wait()
 
 
 def solution(mesh):
@@ -309,9 +307,10 @@
             store_kernel,
             out_shape=(shape(k_cache.shape, BF16), shape(k_cache.shape, BF16), shape((batch, dim), BF16), held, held),
             in_specs=[HBM] + [VMEM] * 5,
-            out_specs=[HBM, HBM, VMEM, VMEM, VMEM],
+            out_specs=[HBM, HBM, HBM, VMEM, VMEM],
             input_output_aliases={1: 3, 2: 4},
-            scratch_shapes=[pltpu.SMEM((batch,), jnp.int32), dma, dma((steps,)), dma((steps,)), dma((2, LOAD_ROWS))],
+            scratch_shapes=[pltpu.SMEM((batch,), jnp.int32), dma, dma, dma((steps,)), dma((steps,)),
+                            dma((2, LOAD_ROWS))],
             compiler_params=pltpu.CompilerParams(vmem_limit_bytes=4 * mib),
         )(hbm[0], k_all, v_all, k_new, v_new, y)
         return y, k_out, v_out

time: 46.4 us -> 44.7 us (0.963)
  Pallas kernels: 45.6 us -> 44 us
    pallas_call x1, Pallas kernels: 33.7 us -> 32.7 us  [local_step(): pl.pallas_call(functools.partial(step_kernel, group), out_shape=(held, he...]
    pallas_call x1, Pallas kernels: 11.9 us -> 11.3 us  [local_step(): pl.pallas_call(store_kernel, out_shape=(shape(k_cache.shape, BF16), shape...]
where the time goes in v9:
time: 44.7 us; the launch traced here: 44.6 us
  Pallas kernels  44 us (98%)
  between operations  0.64 us (1%)
    pallas_call x1, Pallas kernels, local_step(): pl.pallas_call(functools.partial(step_kernel, group), out_shape=(held, he...  32.7 us
    pallas_call x1, Pallas kernels, local_step(): pl.pallas_call(store_kernel, out_shape=(shape(k_cache.shape, BF16), shape...  11.3 us

profile of v9, /device:TPU:0, one launch (start us, length us, event | category | flops | bytes accessed | tf_op | source)
XLA Modules:
  0.0 44.6 jit_solution(7869686129027095882)
XLA Ops:
  0.6 32.7 %shard_map.103 = (bf16[64,512,256]{2,1,0:T(8,128)(2,1)S(1)}, bf16[64,512,256]{2,1,0:T(8,128)(2,1)S(1)}, f32[64,256]{1,0:T(8,128)S(1)}, f32[64,256]{1,0:T(8,128)S(1)}, bf16[512,256]{1,0:T(8,128)(2,1)S(1)}) custom-call(s32[1,512]{1,0:T(1,128)} %bitcast.1, bf16[512,2048]{1,0:T(8,128)(2,1)} %hid_h.1, bf16[2048,256]{1,0:T(8,128)(2,1)} %wq_h.1, ...), custom_call_target="tpu_custom_call" | custom-call | tf_op jit(solution)/shard_map/pallas_call | solution.py:285
  33.3 11.3 %shard_map.104 = (bf16[64,512,256]{2,1,0:T(8,128)(2,1)}, bf16[64,512,256]{2,1,0:T(8,128)(2,1)}, bf16[512,256]{1,0:T(8,128)(2,1)}, bf16[64,512,256]{2,1,0:T(8,128)(2,1)S(1)}, bf16[64,512,256]{2,1,0:T(8,128)(2,1)S(1)}) custom-call(s32[1,512]{1,0:T(1,128)} %bitcast.2, ...), custom_call_target="tpu_custom_call", output_to_operand_aliasing={{3}: (1, {}), {4}: (2, {})} | custom-call | tf_op jit(solution)/shard_map/pallas_call | solution.py:306

commit v10 on v6

--- a/solution.py
+++ b/solution.py
@@ -18,6 +18,7 @@
 LANES = 128
 GROUP = 4
 Q_PARTS = 2
+PEERS = (6, 7, 2, 4, 3, 5, 1)
 
 
 def mm(a, b):
@@ -49,15 +50,20 @@
         return pltpu.make_async_remote_copy(src_ref=src, dst_ref=dst, send_sem=ss, recv_sem=rs,
                                             device_id={'tp': peer}, device_id_type=pl.DeviceIdType.MESH)
 
-    def other(d):
-        return lax.rem(me + d, group)
+    x, y = lax.rem(chip, 2), lax.div(chip, 2)
+
+    def flip(bit, by):
+        return 1 - bit if by else bit
+
+    def other(mask):
+        return flip(y, mask & 4) * 4 + flip(x, mask & 2) * 2 + flip(core, mask & 1)
 
     def load(src, dst, sem, i):
         part = pl.ds(i * LOAD_ROWS, LOAD_ROWS)
         return pltpu.make_async_copy(src.at[part], dst.at[part], sem.at[i])
 
     barrier = pltpu.get_barrier_semaphore()
-    for d in range(1, group):
+    for d in PEERS:
         pl.semaphore_signal(barrier, inc=1, device_id={'tp': other(d)}, device_id_type=pl.DeviceIdType.MESH)
     first = [pltpu.make_async_copy(s, d, h_sem.at[i]) for i, (s, d) in enumerate(
         ((hid_h, hid), (wq_h, wq), (lens_h, lens_v), (lens_h.at[0], lens_s)))]
@@ -85,7 +91,7 @@
     sends = []
     for part in range(Q_PARTS):
         sends.append([])
-        for d in range(1, group):
+        for d in PEERS:
             peer = other(d)
             copy = remote(qrot.at[pl.ds(peer * rows + part * qrows, qrows)], qbuf.at[me, pl.ds(part * qrows, qrows)],
                           q_s.at[part, d], q_r.at[part, d], peer)
@@ -153,7 +159,7 @@
                 part = pl.ds(h * (crows + 1) + half * hrows, hrows)
                 ob[ch, half, h] = jnp.concatenate([of[lane, part, :] for lane in range(2)], axis=-1).astype(BF16)
         copies = []
-        for d in range(1, group):
+        for d in PEERS:
             peer = other(d)
             pc, ph = lax.div(peer, 2), lax.rem(peer, 2)
             copy = remote(ob.at[ch, ph, pl.ds(pc * 2, 2)], obuf.at[ch, :, me], o_s.at[ch, d], o_r.at[ch, d], peer)
@@ -168,7 +174,7 @@
             copy.wait()
         o_own, o_sib = (obuf[ch, p].astype(F32).reshape(heads * hrows, dim).astype(BF16) for p in (core, 1 - core))
         copies = []
-        for d in list(range(1, group)) + [0]:
+        for d in PEERS + (0,):
             peer = other(d)
             cols = pl.ds(pl.multiple_of(peer * dim, dim), dim)
             part = (mm(o_own, wo[:, cols]) + mm(o_sib, wsib[:, cols])).astype(BF16)
@@ -205,7 +211,7 @@
     y_o[...] = yf[...].astype(BF16)
 
 
-def store_kernel(lens_h, k_i, v_i, kn, vn, y_i, k_o, v_o, y_o, k_v, v_v, lens_s, l_sem, k_sem, v_sem, p_sem):
+def store_kernel(lens_h, k_i, v_i, kn, vn, y_i, k_o, v_o, y_o, k_v, v_v, lens_s, l_sem, y_sem, k_sem, v_sem, p_sem):
     rows, seq, dim = k_v.shape
     start = lax.axis_index('tp') * rows
     pairs = ((k_v, k_o, k_sem, kn), (v_v, v_o, v_sem, vn))
@@ -218,7 +224,8 @@
     lens.start()
     for pair in pairs:
         store(pair, 0).start()
-    y_o[...] = y_i[...]
+    y_copy = pltpu.make_async_copy(y_i, y_o, y_sem)
+    y_copy.start()
     slot = lax.broadcasted_iota(jnp.int32, (PATCH, dim), 0)
     lens.wait()
 
@@ -256,6 +263,7 @@
     for p in range(2):
         for b in range(LOAD_ROWS):
             late(p, b).wait()
+    y_copy.wait()
 
 
 def solution(mesh):
@@ -298,9 +306,10 @@
             store_kernel,
             out_shape=(shape(k_cache.shape, BF16), shape(k_cache.shape, BF16), shape((batch, dim), BF16), held, held),
             in_specs=[HBM] + [VMEM] * 5,
-            out_specs=[HBM, HBM, VMEM, VMEM, VMEM],
+            out_specs=[HBM, HBM, HBM, VMEM, VMEM],
             input_output_aliases={1: 3, 2: 4},
-            scratch_shapes=[pltpu.SMEM((batch,), jnp.int32), dma, dma((steps,)), dma((steps,)), dma((2, LOAD_ROWS))],
+            scratch_shapes=[pltpu.SMEM((batch,), jnp.int32), dma, dma, dma((steps,)), dma((steps,)),
+                            dma((2, LOAD_ROWS))],
             compiler_params=pltpu.CompilerParams(vmem_limit_bytes=4 * mib),
         )(hbm[0], k_all, v_all, k_new, v_new, y)
         return y, k_out, v_out

time: 45 us -> 44.6 us (level)
    pallas_call x1, Pallas kernels: 11.9 us -> 11.3 us  [local_step(): pl.pallas_call(store_kernel, out_shape=(shape(k_cache.shape, BF16), shape...]
where the time goes in v10:
time: 44.6 us; the launch traced here: 44.4 us
  Pallas kernels  43.8 us (98%)
  between operations  0.64 us (1%)
    pallas_call x1, Pallas kernels, local_step(): pl.pallas_call(functools.partial(step_kernel, group), out_shape=(held, he...  32.5 us
    pallas_call x1, Pallas kernels, local_step(): pl.pallas_call(store_kernel, out_shape=(shape(k_cache.shape, BF16), shape...  11.3 us

profile of v10, /device:TPU:0, one launch (start us, length us, event | category | flops | bytes accessed | tf_op | source)
XLA Modules:
  0.0 44.4 jit_solution(1270658919388237938)
XLA Ops:
  0.6 32.5 %shard_map.103 = (bf16[64,512,256]{2,1,0:T(8,128)(2,1)S(1)}, bf16[64,512,256]{2,1,0:T(8,128)(2,1)S(1)}, f32[64,256]{1,0:T(8,128)S(1)}, f32[64,256]{1,0:T(8,128)S(1)}, bf16[512,256]{1,0:T(8,128)(2,1)S(1)}) custom-call(s32[1,512]{1,0:T(1,128)} %bitcast.1, bf16[512,2048]{1,0:T(8,128)(2,1)} %hid_h.1, bf16[2048,256]{1,0:T(8,128)(2,1)} %wq_h.1, ...), custom_call_target="tpu_custom_call" | custom-call | tf_op jit(solution)/shard_map/pallas_call | solution.py:284
  33.1 11.3 %shard_map.104 = (bf16[64,512,256]{2,1,0:T(8,128)(2,1)}, bf16[64,512,256]{2,1,0:T(8,128)(2,1)}, bf16[512,256]{1,0:T(8,128)(2,1)}, bf16[64,512,256]{2,1,0:T(8,128)(2,1)S(1)}, bf16[64,512,256]{2,1,0:T(8,128)(2,1)S(1)}) custom-call(s32[1,512]{1,0:T(1,128)} %bitcast.2, ...), custom_call_target="tpu_custom_call", output_to_operand_aliasing={{3}: (1, {}), {4}: (2, {})} | custom-call | tf_op jit(solution)/shard_map/pallas_call | solution.py:305

commit v11 on v10

--- a/solution.py
+++ b/solution.py
@@ -13,11 +13,10 @@
 VMEM = pl.BlockSpec(memory_space=pltpu.VMEM)
 LOAD_ROWS = 8
 CHUNKS = 4
-EARLY = 4
 PATCH = 16
 LANES = 128
 GROUP = 4
-Q_PARTS = 2
+Q_PARTS = 4
 PEERS = (6, 7, 2, 4, 3, 5, 1)
 
 
@@ -61,6 +60,11 @@
     def load(src, dst, sem, i):
         part = pl.ds(i * LOAD_ROWS, LOAD_ROWS)
         return pltpu.make_async_copy(src.at[part], dst.at[part], sem.at[i])
+
+    def wave(ch):
+        for i in range(ch * crows // LOAD_ROWS, (ch + 1) * crows // LOAD_ROWS):
+            load(k_h, k_o, k_sem, i).start()
+            load(v_h, v_o, v_sem, i).start()
 
     barrier = pltpu.get_barrier_semaphore()
     for d in PEERS:
@@ -80,9 +84,7 @@
     sinr[...] = jnp.sin(angles)
     first[0].wait()
     first[1].wait()
-    for i in range(EARLY):
-        load(k_h, k_o, k_sem, i).start()
-        load(v_h, v_o, v_sem, i).start()
+    wave(0)
     q = mm(hid[...], wq[...]).astype(BF16).astype(F32)
     qrot[...] = rope(q, cosr[...], sinr[...]).astype(BF16)
     pl.semaphore_wait(barrier, group - 1)
@@ -100,6 +102,7 @@
     qbuf[me] = qrot[own, :]
     for copy in later:
         copy.wait()
+    wave(1)
     wcopy = remote(wo, wsib, w_s, w_r, chip * 2 + 1 - core)
     wcopy.start()
     mine = hid[own, :]
@@ -116,9 +119,7 @@
                     h, pl.ds(part * qrows, qrows), lane * LANES:(lane + 1) * LANES].astype(F32)
 
     take_q(0)
-    for i in range(EARLY, rows // LOAD_ROWS):
-        load(k_h, k_o, k_sem, i).start()
-        load(v_h, v_o, v_sem, i).start()
+    wave(2)
     slot = lax.broadcasted_iota(jnp.int32, (heads, seq), 1)
 
     def scores(b):
@@ -201,6 +202,8 @@
         if ch and (ch * crows) % qrows == 0:
             take_q(ch * crows // qrows)
         attend_chunk(ch)
+        if ch + 3 < CHUNKS:
+            wave(ch + 3)
         if ch == 0:
             wcopy.wait()
         else:

time: 44.6 us -> 44.4 us (level)
  no operation moved by 1% of the time
where the time goes in v11:
time: 44.4 us; the launch traced here: 44.3 us
  Pallas kernels  43.7 us (98%)
  between operations  0.64 us (1%)
    pallas_call x1, Pallas kernels, local_step(): pl.pallas_call(functools.partial(step_kernel, group), out_shape=(held, he...  32.4 us
    pallas_call x1, Pallas kernels, local_step(): pl.pallas_call(store_kernel, out_shape=(shape(k_cache.shape, BF16), shape...  11.3 us

profile of v11, /device:TPU:0, one launch (start us, length us, event | category | flops | bytes accessed | tf_op | source)
XLA Modules:
  0.0 44.3 jit_solution(5303633995849007517)
XLA Ops:
  0.6 32.4 %shard_map.103 = (bf16[64,512,256]{2,1,0:T(8,128)(2,1)S(1)}, bf16[64,512,256]{2,1,0:T(8,128)(2,1)S(1)}, f32[64,256]{1,0:T(8,128)S(1)}, f32[64,256]{1,0:T(8,128)S(1)}, bf16[512,256]{1,0:T(8,128)(2,1)S(1)}) custom-call(s32[1,512]{1,0:T(1,128)} %bitcast.1, bf16[512,2048]{1,0:T(8,128)(2,1)} %hid_h.1, bf16[2048,256]{1,0:T(8,128)(2,1)} %wq_h.1, ...), custom_call_target="tpu_custom_call" | custom-call | tf_op jit(solution)/shard_map/pallas_call | solution.py:287
  33.0 11.3 %shard_map.104 = (bf16[64,512,256]{2,1,0:T(8,128)(2,1)}, bf16[64,512,256]{2,1,0:T(8,128)(2,1)}, bf16[512,256]{1,0:T(8,128)(2,1)}, bf16[64,512,256]{2,1,0:T(8,128)(2,1)S(1)}, bf16[64,512,256]{2,1,0:T(8,128)(2,1)S(1)}) custom-call(s32[1,512]{1,0:T(1,128)} %bitcast.2, ...), custom_call_target="tpu_custom_call", output_to_operand_aliasing={{3}: (1, {}), {4}: (2, {})} | custom-call | tf_op jit(solution)/shard_map/pallas_call | solution.py:308
